TPU v7x, 32 devices: a whole 2x2x4 slice. The times are simulated.
32 devices in a mesh: px: 4 (over x, core), py: 2 (over y), pz: 4 (over z).
Axes of the slice: x: 2, y: 2, z: 4, core: 2. Of those that a mesh axis runs over, the one named last changes fastest.
Arguments:
- control_values: float32 [28, 14, 28, 512], P('px', 'py', 'pz'), may hold values from -6 to 6
- metric_diag: float32 [3, 32, 512], P(None, 'px', ('py', 'pz')), may hold values from 0.5 to 2
- metric_off: float32 [3, 32, 512], P(None, 'px', ('py', 'pz')), may hold values from -0.2 to 0.2
- mass_weight: float32 [32, 512], P('px', ('py', 'pz')), may hold values from 0.5 to 2
- orient: int32 [4, 2, 4, 3], P('px', 'py', 'pz'), may hold values from 0 to 1
Outputs:
- stiffness_out: float32 [28, 14, 28, 512], P('px', 'py', 'pz')
- mass_out: float32 [28, 14, 28, 512], P('px', 'py', 'pz')
All inputs are finite; a program needn't handle non-finite values.
Results may differ from a plain program's by a relative error of at most 0.0003.
Values sent between devices are 32-bit elements; how exact they have to be, the bound alone decides.
No kernel may reach another device: no remote copies, remote signals or barrier semaphores. Data moves between devices by JAX's collectives and lax.ppermute only.
A program may use at most 64 MiB of HBM per device.

v0:
```python
import functools
import itertools
import math

import jax
import jax.numpy as jnp
import numpy as np
from jax import lax
from jax.experimental import pallas as pl
from jax.experimental.pallas import tpu as pltpu
from jax.sharding import PartitionSpec as P


LANES = 128
ROWS = 8
F32 = jnp.float32
BF16 = jnp.bfloat16


def spline_tables(elements):
    knot_row = np.concatenate(
        [np.zeros(3), np.arange(elements + 1) * 1.0, np.full(3, float(elements))]
    )
    offsets = np.array([0.5 - 0.5 / math.sqrt(3.0), 0.5 + 0.5 / math.sqrt(3.0)])
    points = (np.arange(elements)[:, None] + offsets[None, :]).reshape(-1)
    intervals = np.repeat(np.arange(elements), 2) + 3
    current = np.zeros((points.size, knot_row.size - 1))
    current[np.arange(points.size), intervals] = 1.0
    previous = current
    for degree in range(1, 4):
        columns = knot_row.size - 1 - degree
        updated = np.zeros((points.size, columns))
        for i in range(columns):
            lower_gap = knot_row[i + degree] - knot_row[i]
            upper_gap = knot_row[i + degree + 1] - knot_row[i + 1]
            if lower_gap > 0:
                updated[:, i] += (points - knot_row[i]) / lower_gap * current[:, i]
            if upper_gap > 0:
                updated[:, i] += (knot_row[i + degree + 1] - points) / upper_gap * current[:, i + 1]
        previous = current
        current = updated
    slopes = np.zeros(current.shape)
    for i in range(current.shape[1]):
        lower_gap = knot_row[i + 3] - knot_row[i]
        upper_gap = knot_row[i + 4] - knot_row[i + 1]
        if lower_gap > 0:
            slopes[:, i] += 3.0 / lower_gap * previous[:, i]
        if upper_gap > 0:
            slopes[:, i] -= 3.0 / upper_gap * previous[:, i + 1]
    return (current.astype(np.float32), slopes.astype(np.float32))


def split(x):
    high = x.astype(BF16)
    return high, (x - high.astype(F32)).astype(BF16)


def split_np(x):
    high = x.astype(BF16)
    return high, (x - high.astype(np.float32)).astype(BF16)


def plane_tables(values, slopes):
    quad, ctrl = values.shape

    def pair(left, right):
        table = np.zeros((quad, quad, ROWS, ROWS), np.float32)
        table[:, :, :ctrl, :ctrl] = np.einsum("bj,ck->bcjk", left, right)
        return table.reshape(quad * quad, ROWS * ROWS)

    plain, by_y, by_z = pair(values, values), pair(slopes, values), pair(values, slopes)
    forward = np.concatenate([plain, by_y, by_z])
    high, low = split_np(forward)
    forward = np.concatenate([high, low, high], axis=1)
    zero = np.zeros_like(plain.T)
    back = np.concatenate(
        [
            np.concatenate([plain.T, by_y.T, by_z.T, zero], axis=1)[: ctrl * ROWS],
            np.concatenate([zero, zero, zero, plain.T], axis=1)[: ctrl * ROWS],
        ]
    )
    high, low = split_np(back)
    return forward, np.concatenate([high, low])


def forward_stage(u_ref, w_ref, p_ref, ctrl, arrive):
    vecs = u_ref.shape[-1]
    pad = jnp.zeros((ROWS - ctrl, vecs), F32)
    rest = jnp.zeros(((ROWS - ctrl) * ROWS, vecs), F32)
    for i in range(ctrl):
        arrive(i)
        rows = []
        for j in range(ctrl):
            rows += [u_ref[i, j], pad]
        high, low = split(jnp.concatenate(rows + [rest], axis=0))
        rhs = jnp.concatenate([high, high, low], axis=0)
        p_ref[i] = jnp.dot(w_ref[...], rhs, preferred_element_type=F32)


def metric_stage(diag_ref, off_ref, weight_ref, t_ref):
    quad = weight_ref.shape[0]
    for f in range(3):
        t_ref[f, :, 0:quad] = diag_ref[f].T
        t_ref[3 + f, :, 0:quad] = off_ref[f].T
    t_ref[6, :, 0:quad] = weight_ref[...].T


def point_stage(p_ref, t_ref, m_ref, h_ref, values, slopes, points, outs):
    quad, ctrl = values.shape
    vecs = p_ref.shape[-1]
    area = quad * quad

    def terms(column, table, index):
        total = None
        for i in range(ctrl):
            if table[index, i] != 0.0:
                term = float(table[index, i]) * column[i]
                total = term if total is None else total + term
        return total

    def body(b, carry):
        start = pl.multiple_of(b * quad, quad)
        for f in range(7):
            block = t_ref[f, pl.ds(start, quad), :]
            for a in points:
                m_ref[f * quad + a] = jnp.broadcast_to(block[:, a : a + 1], (quad, LANES))
        for lane in range(0, vecs, LANES):
            cols = pl.ds(lane, LANES)

            def loaded(kind):
                return {i: p_ref[i, pl.ds(pl.multiple_of(kind * area + start, quad), quad), cols] for i in range(ctrl)}

            plain, by_y, by_z = loaded(0), loaded(1), loaded(2)
            sums = [[None] * 4 for _ in outs]

            def gather(n, field, factor, value):
                if factor != 0.0:
                    term = float(factor) * value
                    old = sums[n][field]
                    sums[n][field] = term if old is None else old + term

            for a in points:
                d0, d1, d2, o0, o1, o2, w = (m_ref[f * quad + a] for f in range(7))
                gx = terms(plain, slopes, a)
                gy = terms(by_y, values, a)
                gz = terms(by_z, values, a)
                gp = terms(plain, values, a)
                fx = d0 * gx + o0 * gy + o1 * gz
                fy = o0 * gx + d1 * gy + o2 * gz
                fz = o1 * gx + o2 * gy + d2 * gz
                fm = w * gp
                for n, i in enumerate(outs):
                    gather(n, 0, slopes[a, i], fx)
                    gather(n, 1, values[a, i], fy)
                    gather(n, 2, values[a, i], fz)
                    gather(n, 3, values[a, i], fm)
            for n in range(len(outs)):
                for field in range(4):
                    rows = pl.ds(pl.multiple_of(field * area + start, quad), quad)
                    h_ref[n, rows, cols] = sums[n][field]
        return carry

    lax.fori_loop(0, quad, body, 0)


def back_plane(h, w_ref):
    half = w_ref.shape[0] // 2
    high, low = split(h)
    both = jnp.dot(w_ref[...], high, preferred_element_type=F32)
    return both[:half] + both[half:] + jnp.dot(w_ref[0:half], low, preferred_element_type=F32)


def turned(x, flag, ctrl):
    rows = lax.broadcasted_iota(jnp.int32, x.shape, 0)
    back = jnp.where(rows < ctrl, ctrl - 1 - rows, rows)
    return jnp.take_along_axis(x, jnp.where(flag == 1, back, rows), axis=0, mode="promise_in_bounds")


def at(index, flag, ctrl):
    return jnp.where(flag == 1, ctrl - 1 - index, index)


def body_kernel(values, slopes, flags_in, u_in, diag_in, off_in, weight_in, wf_in, wb_in,
                bulk_ref, xlow_ref, xhigh_ref, dlow_ref, dhigh_ref,
                flags, u_ref, diag_ref, off_ref, weight_ref, wf_ref, wb_ref, u_sems, sems, p_ref, t_ref, m_ref, h_ref):
    quad, ctrl = values.shape
    last = ctrl - 1
    small = [
        pltpu.make_async_copy(src, dst, sems.at[n])
        for n, (src, dst) in enumerate(
            ((wf_in, wf_ref), (diag_in, diag_ref), (off_in, off_ref), (weight_in, weight_ref), (wb_in, wb_ref), (flags_in, flags))
        )
    ]
    planes = [pltpu.make_async_copy(u_in.at[i], u_ref.at[i], u_sems.at[i]) for i in range(ctrl)]
    for copy in small[:1] + planes + small[1:]:
        copy.start()
    small[0].wait()
    forward_stage(u_ref, wf_ref, p_ref, ctrl, lambda i: planes[i].wait())
    for copy in small[1:]:
        copy.wait()
    metric_stage(diag_ref, off_ref, weight_ref, t_ref)
    point_stage(p_ref, t_ref, m_ref, h_ref, values, slopes, range(quad), range(ctrl))
    area = ctrl * ROWS
    lanes = bulk_ref.shape[2]
    for i in range(ctrl):
        both = back_plane(h_ref[i], wb_ref)
        for lane in range(lanes):
            part = both[:, lane * LANES : (lane + 1) * LANES]
            bulk_ref[0, i, lane] = part[:area]
            bulk_ref[1, i, lane] = part[area:]
    fi, fj, fk = flags[0], flags[1], flags[2]
    for field, lane in np.ndindex(2, lanes):
        cols = pl.ds(lane * LANES, LANES)
        for i, x_ref in ((0, xlow_ref), (last, xhigh_ref)):
            here = at(i, fi, ctrl)
            for line, j in ((0, 0), (1, last)):
                x_ref[pl.ds((line * 2 + field) * ctrl, ctrl), cols] = y_line(bulk_ref, field, here, lane, j, flags, ctrl)
            for line, k in ((2, 0), (3, last)):
                x_ref[pl.ds((line * 2 + field) * ctrl, ctrl), cols] = z_line(bulk_ref, field, here, lane, k, flags, ctrl)
        for i, (side, j), (k, d_ref) in itertools.product(range(ctrl), ((0, 0), (1, last)), ((0, dlow_ref), (last, dhigh_ref))):
            row = at(j, fj, ctrl) * ROWS + at(k, fk, ctrl)
            d_ref[pl.ds((side * 2 + field) * ctrl + i, 1), cols] = bulk_ref[field, at(i, fi, ctrl), lane, pl.ds(row, 1), :]


def y_line(bulk_ref, field, here, lane, j, flags, ctrl):
    start = pl.multiple_of(at(j, flags[1], ctrl) * ROWS, ROWS)
    return turned(bulk_ref[field, here, lane, pl.ds(start, ROWS), :], flags[2], ctrl)[0:ctrl]


def z_line(bulk_ref, field, here, lane, k, flags, ctrl):
    block = bulk_ref[field, here, lane, pl.ds(at(k, flags[2], ctrl), ctrl, stride=ROWS), :]
    pad = jnp.zeros((ROWS - ctrl, LANES), F32)
    return turned(jnp.concatenate([block, pad], axis=0), flags[1], ctrl)[0:ctrl]


def pack_kernel(ctrl, flags, bulk_ref, xlow_ref, xhigh_ref, y_ref, zlow_ref, zhigh_ref):
    last = ctrl - 1
    for field, i, lane in np.ndindex(2, ctrl, bulk_ref.shape[2]):
        here = at(i, flags[0], ctrl)
        cols = pl.ds(lane * LANES, LANES)
        x_ref = xlow_ref if i == 0 else xhigh_ref if i == last else None

        def summed(block, line):
            return block if x_ref is None else block + x_ref[pl.ds((line * 2 + field) * ctrl, ctrl), cols]

        for side, j in ((0, 0), (1, last)):
            block = y_line(bulk_ref, field, here, lane, j, flags, ctrl)
            y_ref[pl.ds(((side * 2 + field) * ctrl + i) * ctrl, ctrl), cols] = summed(block, side)
        for side, k, z_ref in ((0, 0, zlow_ref), (1, last, zhigh_ref)):
            block = z_line(bulk_ref, field, here, lane, k, flags, ctrl)
            z_ref[pl.ds((field * ctrl + i) * ctrl, ctrl), cols] = summed(block, 2 + side)


def late_kernel(ctrl, flags, bulk_ref, dlow_ref, dhigh_ref, low_ref, high_ref):
    last = ctrl - 1
    inner = ctrl - 2
    for i, out_ref in ((0, low_ref), (last, high_ref)):
        here = at(i, flags[0], ctrl)
        for field, lane in np.ndindex(2, bulk_ref.shape[2]):
            cols = pl.ds(lane * LANES, LANES)
            for j in range(1, last):
                block = y_line(bulk_ref, field, here, lane, j, flags, ctrl)
                out_ref[pl.ds((field * inner + j - 1) * ctrl, ctrl), cols] = block
        for end, d_ref in enumerate((dlow_ref, dhigh_ref)):
            for side, field in np.ndindex(2, 2):
                row = 2 * inner * ctrl + (end * 2 + side) * 2 + field
                out_ref[pl.ds(row, 1), :] = d_ref[pl.ds((side * 2 + field) * ctrl + i, 1), :]


def join_kernel(ctrl, flags, bulk_ref, xlow_ref, xhigh_ref, llow_ref, lhigh_ref, y_ref, zlow_ref, zhigh_ref,
                dlow_ref, dhigh_ref, k_out, n_out, stage_ref, sems):
    fi, fj, fk = flags[0], flags[1], flags[2]
    last = ctrl - 1
    inner = ctrl - 2
    rows = lax.broadcasted_iota(jnp.int32, (ROWS, LANES), 0)
    at_low, at_high = rows == at(0, fk, ctrl), rows == at(last, fk, ctrl)
    pad = jnp.zeros((ROWS - ctrl, LANES), F32)
    copies = []

    def spread(row):
        return jnp.broadcast_to(row, (ROWS, LANES))

    for i, field in np.ndindex(ctrl, 2):
        here = at(i, fi, ctrl)
        x_ref, l_ref = (xlow_ref, llow_ref) if i == 0 else (xhigh_ref, lhigh_ref) if i == last else (None, None)
        for j, lane in np.ndindex(ctrl, bulk_ref.shape[2]):
            cols = pl.ds(lane * LANES, LANES)
            there = at(j, fj, ctrl)
            rim = 1 if j == 0 else 0 if j == last else None
            block = bulk_ref[field, here, lane, pl.ds(pl.multiple_of(there * ROWS, ROWS), ROWS), :]
            extra = []
            if x_ref is not None:
                if rim is None:
                    extra.append(l_ref[pl.ds((field * inner + j - 1) * ctrl, ctrl), cols])
                else:
                    extra.append(x_ref[pl.ds(((1 - rim) * 2 + field) * ctrl, ctrl), cols])
            if rim is not None:
                extra.append(y_ref[pl.ds(((rim * 2 + field) * ctrl + i) * ctrl, ctrl), cols])
            if extra:
                block = block + turned(jnp.concatenate([sum(extra[1:], extra[0]), pad], axis=0), fk, ctrl)
            ends = []
            for end, (z_ref, d_ref) in enumerate(((zlow_ref, dlow_ref), (zhigh_ref, dhigh_ref))):
                row = z_ref[pl.ds((field * ctrl + i) * ctrl + j, 1), cols]
                if rim is not None:
                    row = row + d_ref[pl.ds((rim * 2 + field) * ctrl + i, 1), cols]
                    if l_ref is not None:
                        row = row + l_ref[pl.ds(2 * inner * ctrl + (end * 2 + rim) * 2 + field, 1), cols]
                ends.append(spread(row))
            block = block + jnp.where(at_low, ends[0], jnp.where(at_high, ends[1], 0.0))
            stage_ref[field, i, there, :, cols] = block[0:ctrl]
        copy = pltpu.make_async_copy(stage_ref.at[field, i], (k_out, n_out)[field].at[here], sems.at[field, i])
        copy.start()
        copies.append(copy)
    for copy in copies:
        copy.wait()


def shifted(x, axes, sizes, steps):
    pairs = []
    for index in np.ndindex(*sizes):
        to = [(p + s) % n for p, s, n in zip(index, steps, sizes)]
        pairs.append((int(np.ravel_multi_index(index, sizes)), int(np.ravel_multi_index(to, sizes))))
    return lax.ppermute(x, axes, pairs)


def per_device(sizes, control_values, metric_diag, metric_off, mass_weight, orient):
    quad = mass_weight.shape[0]
    ctrl, vecs = control_values.shape[0], control_values.shape[-1]
    values, slopes = spline_tables(quad // 2)
    wf_np, wb_np = plane_tables(values, slopes)
    wf, wb = jnp.asarray(wf_np), jnp.asarray(wb_np)
    flags = orient.reshape(3)
    hbm = pl.BlockSpec(memory_space=pltpu.HBM)
    vmem = pl.BlockSpec(memory_space=pltpu.VMEM)
    smem = pl.BlockSpec(memory_space=pltpu.SMEM)
    area = quad * quad
    nx, ny, nz = sizes
    face = 2 * ctrl * ctrl

    def sd(*shape):
        return jax.ShapeDtypeStruct(shape, F32)

    def call(kernel, mib, flops, **kwargs):
        def run(*args):
            return pl.pallas_call(
                kernel,
                compiler_params=pltpu.CompilerParams(vmem_limit_bytes=mib * 2**20),
                cost_estimate=pl.CostEstimate(flops=flops, bytes_accessed=10**6, transcendentals=0),
                **kwargs,
            )(*args)

        return run

    def crossed(pair, axes, counts, *steps):
        if ny == 2:
            return shifted(pair, axes, counts, (1, *steps))
        half = pair.shape[0] // 2
        return jnp.concatenate(
            [shifted(pair[:half], axes, counts, (-1, *steps)), shifted(pair[half:], axes, counts, (1, *steps))]
        )

    yz, yzn = ("py", "pz"), (ny, nz)
    inputs = (flags, control_values, metric_diag, metric_off, mass_weight, wf, wb)
    bulk, xlow, xhigh, dlow, dhigh = call(
        functools.partial(body_kernel, values, slopes),
        20,
        10**9,
        out_shape=[sd(2, ctrl, vecs // LANES, ctrl * ROWS, LANES)] + [sd(8 * ctrl, vecs)] * 2 + [sd(4 * ctrl, vecs)] * 2,
        in_specs=[hbm] * 7,
        out_specs=[vmem] * 5,
        scratch_shapes=[
            pltpu.SMEM((3,), jnp.int32),
            pltpu.VMEM(control_values.shape, F32),
            pltpu.VMEM(metric_diag.shape, F32),
            pltpu.VMEM(metric_off.shape, F32),
            pltpu.VMEM(mass_weight.shape, F32),
            pltpu.VMEM(wf.shape, BF16),
            pltpu.VMEM(wb.shape, BF16),
            pltpu.SemaphoreType.DMA((ctrl,)),
            pltpu.SemaphoreType.DMA((6,)),
            pltpu.VMEM((ctrl, 3 * area, vecs), F32),
            pltpu.VMEM((7, area, LANES), F32),
            pltpu.VMEM((7 * quad, quad, LANES), F32),
            pltpu.VMEM((ctrl, 4 * area, vecs), F32),
        ],
    )(*(pltpu.with_memory_space_constraint(x, pltpu.HBM) for x in inputs))
    xlow_in = shifted(xhigh, ("px",), (nx,), (1,))
    xhigh_in = shifted(xlow, ("px",), (nx,), (-1,))
    dlow_in = crossed(dhigh, yz, yzn, 1)
    dhigh_in = crossed(dlow, yz, yzn, -1)
    ysend, zlow, zhigh = call(
        functools.partial(pack_kernel, ctrl),
        8,
        10**8,
        out_shape=[sd(2 * face, vecs)] + [sd(face, vecs)] * 2,
        in_specs=[smem] + [vmem] * 3,
        out_specs=[vmem] * 3,
    )(flags, bulk, xlow_in, xhigh_in)
    zlow_in = shifted(zhigh, ("pz",), (nz,), (1,))
    y_in = crossed(ysend, ("py",), (ny,))
    zhigh_in = shifted(zlow, ("pz",), (nz,), (-1,))
    late = 2 * (ctrl - 2) * ctrl + 8
    llow, lhigh = call(
        functools.partial(late_kernel, ctrl),
        8,
        10**7,
        out_shape=[sd(late, vecs)] * 2,
        in_specs=[smem] + [vmem] * 3,
        out_specs=[vmem] * 2,
    )(flags, bulk, dlow_in, dhigh_in)
    llow_in = shifted(lhigh, ("px",), (nx,), (1,))
    lhigh_in = shifted(llow, ("px",), (nx,), (-1,))
    return tuple(
        call(
            functools.partial(join_kernel, ctrl),
            10,
            10**8,
            out_shape=[sd(*control_values.shape)] * 2,
            in_specs=[smem] + [vmem] * 10,
            out_specs=[hbm] * 2,
            scratch_shapes=[pltpu.VMEM((2, *control_values.shape), F32), pltpu.SemaphoreType.DMA((2, ctrl))],
        )(flags, bulk, xlow_in, xhigh_in, llow_in, lhigh_in, y_in, zlow_in, zhigh_in, dlow_in, dhigh_in)
    )


def solution(mesh):
    in_specs = (
        P("px", "py", "pz", None),
        P(None, "px", ("py", "pz")),
        P(None, "px", ("py", "pz")),
        P("px", ("py", "pz")),
        P("px", "py", "pz", None),
    )
    out_specs = (P("px", "py", "pz", None), P("px", "py", "pz", None))
    sizes = (mesh.shape["px"], mesh.shape["py"], mesh.shape["pz"])

    def body(*args):
        return per_device(sizes, *args)

    return jax.shard_map(body, mesh=mesh, in_specs=in_specs, out_specs=out_specs, check_vma=False)
```

profile of v0, /device:TPU:0, one launch (start us, length us, event | category | flops | bytes accessed | tf_op | source)
XLA Modules:
  0.0 35.2 jit_solution(16464302676947301983)
XLA Ops:
  0.6 0.0 copy-start
  0.6 6.9 %shard_map.86 = (f32[2,7,4,56,128]{4,3,2,1,0:T(8,128)S(1)}, f32[56,512]{1,0:T(8,128)S(1)}, f32[56,512]{1,0:T(8,128)S(1)}, f32[28,512]{1,0:T(8,128)S(1)}, f32[28,512]{1,0:T(8,128)S(1)}) custom-call(s32[3]{0:T(128)} %bitcast.1, f32[7,7,7,512]{3,2,1,0:T(8,128)} %u_in.1, f32[3,8,64]{2,1,0:T(8,128)} %diag_in.1, f32[3,8,64]{2,1,0:T(8,128)} %off_in.1, ...), custom_call_target="tpu_custom_call" | custom-call | flops 1000000000 | bytes 1000000 | tf_op jit(solution)/shard_map/pallas_call | solution.py:345
  7.5 0.5 %collective-permute-start = (f32[56,512]{1,0:T(8,128)S(1)}, f32[56,512]{1,0:T(8,128)S(1)}, u32[]{:S(2)}, u32[]{:S(2)}) collective-permute-start(f32[56,512]{1,0:T(8,128)S(1)} %get-tuple-element.13), channel_id=1, source_target_pairs={{0,8},{8,16},{16,24},{24,0},{1,9},{9,17},{17,25},{25,1},{2,10},{10... | collective-permute-start | bytes 344072 | tf_op jit(solution)/shard_map/ppermute | solution.py:323
  8.1 2.0 %collective-permute-start.1 = (f32[56,512]{1,0:T(8,128)S(1)}, f32[56,512]{1,0:T(8,128)S(1)}, u32[]{:S(2)}, u32[]{:S(2)}) collective-permute-start(f32[56,512]{1,0:T(8,128)S(1)} %get-tuple-element.14), channel_id=1, source_target_pairs={{0,24},{8,0},{16,8},{24,16},{1,25},{9,1},{17,9},{25,17},{2,26},{10... | collective-permute-start | bytes 344072 | tf_op jit(solution)/shard_map/ppermute | solution.py:323
  10.0 2.4 %collective-permute-done.xlow_ref = f32[56,512]{1,0:T(8,128)S(1)} collective-permute-done((f32[56,512]{1,0:T(8,128)S(1)}, f32[56,512]{1,0:T(8,128)S(1)}, u32[]{:S(2)}, u32[]{:S(2)}) %collective-permute-start) | collective-permute-done | bytes 114720 | tf_op jit(solution)/shard_map/ppermute | solution.py:323
  12.5 1.0 %collective-permute-done.1.xhigh_ref = f32[56,512]{1,0:T(8,128)S(1)} collective-permute-done((f32[56,512]{1,0:T(8,128)S(1)}, f32[56,512]{1,0:T(8,128)S(1)}, u32[]{:S(2)}, u32[]{:S(2)}) %collective-permute-start.1) | collective-permute-done | bytes 114720 | tf_op jit(solution)/shard_map/ppermute | solution.py:323
  13.5 0.0 copy-done
  13.5 0.8 %shard_map.88 = (f32[196,512]{1,0:T(8,128)S(1)}, f32[98,512]{1,0:T(8,128)S(1)}, f32[98,512]{1,0:T(8,128)S(1)}) custom-call(s32[3]{0:T(128)S(1)} %bitcast.2, f32[2,7,4,56,128]{4,3,2,1,0:T(8,128)S(1)} %get-tuple-element.12.bulk_ref, f32[56,512]{1,0:T(8,128)S(1)} %collective-permute-done.xlow_ref, f32[56,512]{1,0:T(8,128)S(1)} %collective-permute-done.1.xhigh_ref), custom_call_target="tpu_custom_call" | custom-call | flops 100000000 | bytes 1000000 | tf_op jit(solution)/shard_map/pallas_call | solution.py:345
  14.3 1.6 %collective-permute-start.6 = (f32[196,512]{1,0:T(8,128)S(1)}, f32[196,512]{1,0:T(8,128)S(1)}, u32[]{:S(2)}, u32[]{:S(2)}) collective-permute-start(f32[196,512]{1,0:T(8,128)S(1)} %get-tuple-element.19), channel_id=1, source_target_pairs={{0,4},{4,0},{1,5},{5,1},{2,6},{6,2},{3,7},{7,3},{8,12},{12,8},{9,1... | collective-permute-start | bytes 1204232 | tf_op jit(solution)/shard_map/ppermute | solution.py:323
  15.9 1.5 %collective-permute-start.2 = (f32[28,512]{1,0:T(8,128)S(1)}, f32[28,512]{1,0:T(8,128)S(1)}, u32[]{:S(2)}, u32[]{:S(2)}) collective-permute-start(f32[28,512]{1,0:T(8,128)S(1)} %get-tuple-element.15), channel_id=1, source_target_pairs={{0,5},{1,6},{2,7},{3,4},{4,1},{5,2},{6,3},{7,0},{8,13},{9,14},{10,... | collective-permute-start | bytes 172040 | tf_op jit(solution)/shard_map/ppermute | solution.py:323
  17.4 3.2 %collective-permute-start.3 = (f32[28,512]{1,0:T(8,128)S(1)}, f32[28,512]{1,0:T(8,128)S(1)}, u32[]{:S(2)}, u32[]{:S(2)}) collective-permute-start(f32[28,512]{1,0:T(8,128)S(1)} %get-tuple-element.16), channel_id=1, source_target_pairs={{0,7},{1,4},{2,5},{3,6},{4,3},{5,0},{6,1},{7,2},{8,15},{9,12},{10,... | collective-permute-start | bytes 172040 | tf_op jit(solution)/shard_map/ppermute | solution.py:323
  20.6 0.0 collective-permute-start.7
  20.6 3.8 %collective-permute-start.8 = (f32[98,512]{1,0:T(8,128)S(1)}, f32[98,512]{1,0:T(8,128)S(1)}, u32[]{:S(2)}, u32[]{:S(2)}) collective-permute-start(f32[98,512]{1,0:T(8,128)S(1)} %get-tuple-element.21), channel_id=1, source_target_pairs={{0,3},{1,0},{2,1},{3,2},{4,7},{5,4},{6,5},{7,6},{8,11},{9,8},{10,9... | collective-permute-start | bytes 602120 | tf_op jit(solution)/shard_map/ppermute | solution.py:323
  24.5 0.0 collective-permute-done.2.dlow_ref
  24.5 0.3 collective-permute-done.3.dhigh_ref
  24.7 0.6 %shard_map.87 = (f32[78,512]{1,0:T(8,128)S(1)}, f32[78,512]{1,0:T(8,128)S(1)}) custom-call(s32[3]{0:T(128)S(1)} %bitcast.3, f32[2,7,4,56,128]{4,3,2,1,0:T(8,128)S(1)} %get-tuple-element.12.bulk_ref, f32[28,512]{1,0:T(8,128)S(1)} %collective-permute-done.2.dlow_ref, f32[28,512]{1,0:T(8,128)S(1)} %collective-permute-done.3.dhigh_ref), custom_call_target="tpu_custom_call" | custom-call | flops 10000000 | bytes 1000000 | tf_op jit(solution)/shard_map/pallas_call | solution.py:345
  25.4 0.1 collective-permute-start.4
  25.4 1.7 %collective-permute-start.5 = (f32[78,512]{1,0:T(8,128)S(1)}, f32[78,512]{1,0:T(8,128)S(1)}, u32[]{:S(2)}, u32[]{:S(2)}) collective-permute-start(f32[78,512]{1,0:T(8,128)S(1)} %get-tuple-element.18), channel_id=1, source_target_pairs={{0,24},{8,0},{16,8},{24,16},{1,25},{9,1},{17,9},{25,17},{2,26},{10... | collective-permute-start | bytes 479240 | tf_op jit(solution)/shard_map/ppermute | solution.py:323
  27.2 3.0 %collective-permute-done.4.llow_ref = f32[78,512]{1,0:T(8,128)S(1)} collective-permute-done((f32[78,512]{1,0:T(8,128)S(1)}, f32[78,512]{1,0:T(8,128)S(1)}, u32[]{:S(2)}, u32[]{:S(2)}) %collective-permute-start.4) | collective-permute-done | bytes 159776 | tf_op jit(solution)/shard_map/ppermute | solution.py:323
  30.2 0.7 %collective-permute-done.5.lhigh_ref = f32[78,512]{1,0:T(8,128)S(1)} collective-permute-done((f32[78,512]{1,0:T(8,128)S(1)}, f32[78,512]{1,0:T(8,128)S(1)}, u32[]{:S(2)}, u32[]{:S(2)}) %collective-permute-start.5) | collective-permute-done | bytes 159776 | tf_op jit(solution)/shard_map/ppermute | solution.py:323
  30.9 0.0 collective-permute-done.7.zlow_ref
  30.9 2.3 %collective-permute-done.8.zhigh_ref = f32[98,512]{1,0:T(8,128)S(1)} collective-permute-done((f32[98,512]{1,0:T(8,128)S(1)}, f32[98,512]{1,0:T(8,128)S(1)}, u32[]{:S(2)}, u32[]{:S(2)}) %collective-permute-start.8) | collective-permute-done | bytes 200736 | tf_op jit(solution)/shard_map/ppermute | solution.py:323
  33.2 0.0 collective-permute-done.6.y_ref
  33.2 2.0 %shard_map.89 = (f32[7,7,7,512]{3,2,1,0:T(8,128)}, f32[7,7,7,512]{3,2,1,0:T(8,128)}) custom-call(s32[3]{0:T(128)S(1)} %bitcast.4, f32[2,7,4,56,128]{4,3,2,1,0:T(8,128)S(1)} %get-tuple-element.12.bulk_ref, f32[56,512]{1,0:T(8,128)S(1)} %collective-permute-done.xlow_ref, f32[56,512]{1,0:T(8,128)S(1)} %collective-permute-done.1.xhigh_ref, ...), custom_call_target="tpu_custom_call" | custom-call | flops 100000000 | bytes 1000000 | tf_op jit(solution)/shard_map/pallas_call | solution.py:345
Async XLA Ops:
  0.6 12.9 %copy-start = (s32[1,1,1,3]{3,2,1,0:T(1,128)S(1)}, s32[1,1,1,3]{3,2,1,0:T(1,128)}, u32[]{:S(2)}) copy-start(s32[1,1,1,3]{3,2,1,0:T(1,128)} %param.11) | copy-start | bytes 40
  7.5 4.9 %collective-permute-start = (f32[56,512]{1,0:T(8,128)S(1)}, f32[56,512]{1,0:T(8,128)S(1)}, u32[]{:S(2)}, u32[]{:S(2)}) collective-permute-start(f32[56,512]{1,0:T(8,128)S(1)} %get-tuple-element.13), channel_id=1, source_target_pairs={{0,8},{8,16},{16,24},{24,0},{1,9},{9,17},{17,25},{25,1},{2,10},{10... | collective-permute-start | bytes 344072 | tf_op jit(solution)/shard_map/ppermute | solution.py:323
  8.1 5.4 %collective-permute-start.1 = (f32[56,512]{1,0:T(8,128)S(1)}, f32[56,512]{1,0:T(8,128)S(1)}, u32[]{:S(2)}, u32[]{:S(2)}) collective-permute-start(f32[56,512]{1,0:T(8,128)S(1)} %get-tuple-element.14), channel_id=1, source_target_pairs={{0,24},{8,0},{16,8},{24,16},{1,25},{9,1},{17,9},{25,17},{2,26},{10... | collective-permute-start | bytes 344072 | tf_op jit(solution)/shard_map/ppermute | solution.py:323
  14.3 18.9 %collective-permute-start.6 = (f32[196,512]{1,0:T(8,128)S(1)}, f32[196,512]{1,0:T(8,128)S(1)}, u32[]{:S(2)}, u32[]{:S(2)}) collective-permute-start(f32[196,512]{1,0:T(8,128)S(1)} %get-tuple-element.19), channel_id=1, source_target_pairs={{0,4},{4,0},{1,5},{5,1},{2,6},{6,2},{3,7},{7,3},{8,12},{12,8},{9,1... | collective-permute-start | bytes 1204232 | tf_op jit(solution)/shard_map/ppermute | solution.py:323
  15.9 8.6 %collective-permute-start.2 = (f32[28,512]{1,0:T(8,128)S(1)}, f32[28,512]{1,0:T(8,128)S(1)}, u32[]{:S(2)}, u32[]{:S(2)}) collective-permute-start(f32[28,512]{1,0:T(8,128)S(1)} %get-tuple-element.15), channel_id=1, source_target_pairs={{0,5},{1,6},{2,7},{3,4},{4,1},{5,2},{6,3},{7,0},{8,13},{9,14},{10,... | collective-permute-start | bytes 172040 | tf_op jit(solution)/shard_map/ppermute | solution.py:323
  17.4 7.3 %collective-permute-start.3 = (f32[28,512]{1,0:T(8,128)S(1)}, f32[28,512]{1,0:T(8,128)S(1)}, u32[]{:S(2)}, u32[]{:S(2)}) collective-permute-start(f32[28,512]{1,0:T(8,128)S(1)} %get-tuple-element.16), channel_id=1, source_target_pairs={{0,7},{1,4},{2,5},{3,6},{4,3},{5,0},{6,1},{7,2},{8,15},{9,12},{10,... | collective-permute-start | bytes 172040 | tf_op jit(solution)/shard_map/ppermute | solution.py:323
  20.6 10.2 %collective-permute-start.7 = (f32[98,512]{1,0:T(8,128)S(1)}, f32[98,512]{1,0:T(8,128)S(1)}, u32[]{:S(2)}, u32[]{:S(2)}) collective-permute-start(f32[98,512]{1,0:T(8,128)S(1)} %get-tuple-element.20), channel_id=1, source_target_pairs={{0,1},{1,2},{2,3},{3,0},{4,5},{5,6},{6,7},{7,4},{8,9},{9,10},{10,1... | collective-permute-start | bytes 602120 | tf_op jit(solution)/shard_map/ppermute | solution.py:323
  20.6 12.5 %collective-permute-start.8 = (f32[98,512]{1,0:T(8,128)S(1)}, f32[98,512]{1,0:T(8,128)S(1)}, u32[]{:S(2)}, u32[]{:S(2)}) collective-permute-start(f32[98,512]{1,0:T(8,128)S(1)} %get-tuple-element.21), channel_id=1, source_target_pairs={{0,3},{1,0},{2,1},{3,2},{4,7},{5,4},{6,5},{7,6},{8,11},{9,8},{10,9... | collective-permute-start | bytes 602120 | tf_op jit(solution)/shard_map/ppermute | solution.py:323
  25.4 4.8 %collective-permute-start.4 = (f32[78,512]{1,0:T(8,128)S(1)}, f32[78,512]{1,0:T(8,128)S(1)}, u32[]{:S(2)}, u32[]{:S(2)}) collective-permute-start(f32[78,512]{1,0:T(8,128)S(1)} %get-tuple-element.17), channel_id=1, source_target_pairs={{0,8},{8,16},{16,24},{24,0},{1,9},{9,17},{17,25},{25,1},{2,10},{10... | collective-permute-start | bytes 479240 | tf_op jit(solution)/shard_map/ppermute | solution.py:323
  25.4 5.4 %collective-permute-start.5 = (f32[78,512]{1,0:T(8,128)S(1)}, f32[78,512]{1,0:T(8,128)S(1)}, u32[]{:S(2)}, u32[]{:S(2)}) collective-permute-start(f32[78,512]{1,0:T(8,128)S(1)} %get-tuple-element.18), channel_id=1, source_target_pairs={{0,24},{8,0},{16,8},{24,16},{1,25},{9,1},{17,9},{25,17},{2,26},{10... | collective-permute-start | bytes 479240 | tf_op jit(solution)/shard_map/ppermute | solution.py:323
where the time goes:
time: 35.3 us; the launch traced here: 35.2 us
  starting transfers between devices  14.5 us (41%)
  Pallas kernels  10.3 us (29%)
  waiting for transfers between devices  9.77 us (28%)
  between operations  0.67 us (2%)
    ppermute x9, starting transfers between devices, shifted(): return lax.ppermute(x, axes, pairs)  14.5 us
    pallas_call x4, Pallas kernels, run(): pl.pallas_call(kernel, compiler_params=pltpu.CompilerParams(vmem_limit_by...  10.3 us
    ppermute x9, waiting for transfers between devices, shifted(): return lax.ppermute(x, axes, pairs)  9.77 us
  transfers between devices with their start and end apart: 9, of which 6 were waited for; matrix products, arithmetic and copies ran while one was open for 0% of the time, Pallas kernels for 2%

commit v1 on v0

--- a/solution.py
+++ b/solution.py
@@ -69,32 +69,62 @@
         return table.reshape(quad * quad, ROWS * ROWS)
 
     plain, by_y, by_z = pair(values, values), pair(slopes, values), pair(values, slopes)
-    forward = np.concatenate([plain, by_y, by_z])
-    high, low = split_np(forward)
+    high, low = split_np(np.concatenate([plain, by_y, by_z]))
     forward = np.concatenate([high, low, high], axis=1)
     zero = np.zeros_like(plain.T)
+    used = ctrl * ROWS
     back = np.concatenate(
         [
-            np.concatenate([plain.T, by_y.T, by_z.T, zero], axis=1)[: ctrl * ROWS],
-            np.concatenate([zero, zero, zero, plain.T], axis=1)[: ctrl * ROWS],
+            np.concatenate([plain.T, zero, zero, zero], axis=1)[:used],
+            np.concatenate([zero, by_y.T, by_z.T, zero], axis=1)[:used],
+            np.concatenate([zero, zero, zero, plain.T], axis=1)[:used],
         ]
     )
     high, low = split_np(back)
-    return forward, np.concatenate([high, low])
-
-
-def forward_stage(u_ref, w_ref, p_ref, ctrl, arrive):
+    return forward, np.concatenate([high, low, high], axis=1)
+
+
+def terms(table, index, column):
+    total = None
+    for n in range(table.shape[1]):
+        if table[index, n] != 0.0:
+            term = float(table[index, n]) * column(n)
+            total = term if total is None else total + term
+    return total
+
+
+def operand_stage(a, u_ref, v_ref, values, slopes):
+    ctrl = values.shape[1]
     vecs = u_ref.shape[-1]
-    pad = jnp.zeros((ROWS - ctrl, vecs), F32)
-    rest = jnp.zeros(((ROWS - ctrl) * ROWS, vecs), F32)
-    for i in range(ctrl):
-        arrive(i)
-        rows = []
-        for j in range(ctrl):
-            rows += [u_ref[i, j], pad]
-        high, low = split(jnp.concatenate(rows + [rest], axis=0))
-        rhs = jnp.concatenate([high, high, low], axis=0)
-        p_ref[i] = jnp.dot(w_ref[...], rhs, preferred_element_type=F32)
+    pair = 2 * ROWS
+    area = ROWS * ROWS
+    for lane in range(0, vecs, LANES):
+        cols = slice(lane, lane + LANES)
+        for j in range(0, ROWS, 2):
+            tiles = {}
+
+            def column(i, j):
+                if (i, j) not in tiles:
+                    tiles[i, j] = u_ref[i, j, :, cols]
+                return tiles[i, j]
+
+            for n, table in enumerate((slopes, values)):
+                rows = []
+                for k in range(j, min(j + 2, ctrl)):
+                    rows += [terms(table, a, lambda i: column(i, k)), jnp.zeros((ROWS - ctrl, LANES), F32)]
+                if j + 2 > ctrl:
+                    rows.append(jnp.zeros(((j + 2 - ctrl) * ROWS, LANES), F32))
+                high, low = split(jnp.concatenate(rows, axis=0))
+                for part, block in enumerate((high, high, low)):
+                    v_ref[a, n, part * area + j * ROWS : part * area + j * ROWS + pair, cols] = block
+
+
+def gradient_stage(a, v_ref, wf_ref, g_ref):
+    area = wf_ref.shape[0] // 3
+    g_ref[a, 0:area] = jnp.dot(wf_ref[0:area], v_ref[a, 0], preferred_element_type=F32)
+    plane = jnp.dot(wf_ref[...], v_ref[a, 1], preferred_element_type=F32)
+    g_ref[a, area : 3 * area] = plane[area:]
+    g_ref[a, 3 * area :] = plane[0:area]
 
 
 def metric_stage(diag_ref, off_ref, weight_ref, t_ref):
@@ -105,69 +135,59 @@
     t_ref[6, :, 0:quad] = weight_ref[...].T
 
 
-def point_stage(p_ref, t_ref, m_ref, h_ref, values, slopes, points, outs):
-    quad, ctrl = values.shape
-    vecs = p_ref.shape[-1]
-    area = quad * quad
-
-    def terms(column, table, index):
-        total = None
+def flux_stage(a, g_ref, t_ref, f_ref):
+    area, vecs = t_ref.shape[1], g_ref.shape[-1]
+    pair = 2 * ROWS
+    for start in range(0, area, pair):
+        d0, d1, d2, o0, o1, o2, w = (
+            jnp.broadcast_to(t_ref[f, start : start + pair, a : a + 1], (pair, LANES)) for f in range(7)
+        )
+        for lane in range(0, vecs, LANES):
+            cols = slice(lane, lane + LANES)
+            gx, gy, gz, gp = (g_ref[a, n * area + start : n * area + start + pair, cols] for n in range(4))
+            fluxes = (
+                d0 * gx + o0 * gy + o1 * gz,
+                o0 * gx + d1 * gy + o2 * gz,
+                o1 * gx + o2 * gy + d2 * gz,
+                w * gp,
+            )
+            for n, flux in enumerate(fluxes):
+                high, low = split(flux)
+                f_ref[a, n * area + start : n * area + start + pair, cols] = high
+                f_ref[a, (4 + n) * area + start : (4 + n) * area + start + pair, cols] = low
+
+
+def back_stage(a, f_ref, wb_ref, x_ref):
+    half = f_ref.shape[1] // 2
+    high, low = f_ref[a, 0:half], f_ref[a, half:]
+    x_ref[a] = jnp.dot(wb_ref[...], jnp.concatenate([high, high, low], axis=0), preferred_element_type=F32)
+
+
+def last_stage(x_ref, bulk_ref, values, slopes):
+    ctrl = values.shape[1]
+    area = ctrl * ROWS
+    for j, lane in np.ndindex(ctrl, bulk_ref.shape[2]):
+        cols = slice(lane * LANES, (lane + 1) * LANES)
+
+        def block(kind):
+            loaded = {}
+
+            def at_plane(a):
+                if a not in loaded:
+                    loaded[a] = x_ref[a, kind * area + j * ROWS : kind * area + (j + 1) * ROWS, cols]
+                return loaded[a]
+
+            return at_plane
+
+        by_x, by_rest, mass = block(0), block(1), block(2)
         for i in range(ctrl):
-            if table[index, i] != 0.0:
-                term = float(table[index, i]) * column[i]
-                total = term if total is None else total + term
-        return total
-
-    def body(b, carry):
-        start = pl.multiple_of(b * quad, quad)
-        for f in range(7):
-            block = t_ref[f, pl.ds(start, quad), :]
-            for a in points:
-                m_ref[f * quad + a] = jnp.broadcast_to(block[:, a : a + 1], (quad, LANES))
-        for lane in range(0, vecs, LANES):
-            cols = pl.ds(lane, LANES)
-
-            def loaded(kind):
-                return {i: p_ref[i, pl.ds(pl.multiple_of(kind * area + start, quad), quad), cols] for i in range(ctrl)}
-
-            plain, by_y, by_z = loaded(0), loaded(1), loaded(2)
-            sums = [[None] * 4 for _ in outs]
-
-            def gather(n, field, factor, value):
-                if factor != 0.0:
-                    term = float(factor) * value
-                    old = sums[n][field]
-                    sums[n][field] = term if old is None else old + term
-
-            for a in points:
-                d0, d1, d2, o0, o1, o2, w = (m_ref[f * quad + a] for f in range(7))
-                gx = terms(plain, slopes, a)
-                gy = terms(by_y, values, a)
-                gz = terms(by_z, values, a)
-                gp = terms(plain, values, a)
-                fx = d0 * gx + o0 * gy + o1 * gz
-                fy = o0 * gx + d1 * gy + o2 * gz
-                fz = o1 * gx + o2 * gy + d2 * gz
-                fm = w * gp
-                for n, i in enumerate(outs):
-                    gather(n, 0, slopes[a, i], fx)
-                    gather(n, 1, values[a, i], fy)
-                    gather(n, 2, values[a, i], fz)
-                    gather(n, 3, values[a, i], fm)
-            for n in range(len(outs)):
-                for field in range(4):
-                    rows = pl.ds(pl.multiple_of(field * area + start, quad), quad)
-                    h_ref[n, rows, cols] = sums[n][field]
-        return carry
-
-    lax.fori_loop(0, quad, body, 0)
-
-
-def back_plane(h, w_ref):
-    half = w_ref.shape[0] // 2
-    high, low = split(h)
-    both = jnp.dot(w_ref[...], high, preferred_element_type=F32)
-    return both[:half] + both[half:] + jnp.dot(w_ref[0:half], low, preferred_element_type=F32)
+            bulk_ref[0, i, lane, j * ROWS : (j + 1) * ROWS] = terms(slopes.T, i, by_x) + terms(values.T, i, by_rest)
+            bulk_ref[1, i, lane, j * ROWS : (j + 1) * ROWS] = terms(values.T, i, mass)
+
+
+def scalars(flags_ref):
+    flags = flags_ref[...]
+    return [flags[0, d] for d in range(flags.shape[1])]
 
 
 def turned(x, flag, ctrl):
@@ -182,33 +202,35 @@
 
 def body_kernel(values, slopes, flags_in, u_in, diag_in, off_in, weight_in, wf_in, wb_in,
                 bulk_ref, xlow_ref, xhigh_ref, dlow_ref, dhigh_ref,
-                flags, u_ref, diag_ref, off_ref, weight_ref, wf_ref, wb_ref, u_sems, sems, p_ref, t_ref, m_ref, h_ref):
+                flags_ref, u_ref, diag_ref, off_ref, weight_ref, wf_ref, wb_ref, u_sems, sems, t_ref, v_ref, g_ref, f_ref, x_ref):
     quad, ctrl = values.shape
     last = ctrl - 1
     small = [
         pltpu.make_async_copy(src, dst, sems.at[n])
         for n, (src, dst) in enumerate(
-            ((wf_in, wf_ref), (diag_in, diag_ref), (off_in, off_ref), (weight_in, weight_ref), (wb_in, wb_ref), (flags_in, flags))
+            ((wf_in, wf_ref), (diag_in, diag_ref), (off_in, off_ref), (weight_in, weight_ref), (wb_in, wb_ref), (flags_in, flags_ref))
         )
     ]
     planes = [pltpu.make_async_copy(u_in.at[i], u_ref.at[i], u_sems.at[i]) for i in range(ctrl)]
-    for copy in small[:1] + planes + small[1:]:
+    for copy in small[1:4] + planes + small[:1] + small[4:]:
         copy.start()
-    small[0].wait()
-    forward_stage(u_ref, wf_ref, p_ref, ctrl, lambda i: planes[i].wait())
-    for copy in small[1:]:
+    for copy in small[1:4]:
         copy.wait()
     metric_stage(diag_ref, off_ref, weight_ref, t_ref)
-    point_stage(p_ref, t_ref, m_ref, h_ref, values, slopes, range(quad), range(ctrl))
-    area = ctrl * ROWS
+    for copy in planes + small[:1] + small[4:]:
+        copy.wait()
+    for step in range(quad + 2):
+        if step < quad:
+            operand_stage(step, u_ref, v_ref, values, slopes)
+            gradient_stage(step, v_ref, wf_ref, g_ref)
+        if 0 <= step - 1 < quad:
+            flux_stage(step - 1, g_ref, t_ref, f_ref)
+        if 0 <= step - 2 < quad:
+            back_stage(step - 2, f_ref, wb_ref, x_ref)
+    last_stage(x_ref, bulk_ref, values, slopes)
     lanes = bulk_ref.shape[2]
-    for i in range(ctrl):
-        both = back_plane(h_ref[i], wb_ref)
-        for lane in range(lanes):
-            part = both[:, lane * LANES : (lane + 1) * LANES]
-            bulk_ref[0, i, lane] = part[:area]
-            bulk_ref[1, i, lane] = part[area:]
-    fi, fj, fk = flags[0], flags[1], flags[2]
+    flags = scalars(flags_ref)
+    fi, fj, fk = flags
     for field, lane in np.ndindex(2, lanes):
         cols = pl.ds(lane * LANES, LANES)
         for i, x_ref in ((0, xlow_ref), (last, xhigh_ref)):
@@ -233,7 +255,8 @@
     return turned(jnp.concatenate([block, pad], axis=0), flags[1], ctrl)[0:ctrl]
 
 
-def pack_kernel(ctrl, flags, bulk_ref, xlow_ref, xhigh_ref, y_ref, zlow_ref, zhigh_ref):
+def pack_kernel(ctrl, flags_ref, bulk_ref, xlow_ref, xhigh_ref, y_ref, zlow_ref, zhigh_ref):
+    flags = scalars(flags_ref)
     last = ctrl - 1
     for field, i, lane in np.ndindex(2, ctrl, bulk_ref.shape[2]):
         here = at(i, flags[0], ctrl)
@@ -251,7 +274,8 @@
             z_ref[pl.ds((field * ctrl + i) * ctrl, ctrl), cols] = summed(block, 2 + side)
 
 
-def late_kernel(ctrl, flags, bulk_ref, dlow_ref, dhigh_ref, low_ref, high_ref):
+def late_kernel(ctrl, flags_ref, bulk_ref, dlow_ref, dhigh_ref, low_ref, high_ref):
+    flags = scalars(flags_ref)
     last = ctrl - 1
     inner = ctrl - 2
     for i, out_ref in ((0, low_ref), (last, high_ref)):
@@ -267,9 +291,9 @@
                 out_ref[pl.ds(row, 1), :] = d_ref[pl.ds((side * 2 + field) * ctrl + i, 1), :]
 
 
-def join_kernel(ctrl, flags, bulk_ref, xlow_ref, xhigh_ref, llow_ref, lhigh_ref, y_ref, zlow_ref, zhigh_ref,
+def join_kernel(ctrl, flags_ref, bulk_ref, xlow_ref, xhigh_ref, llow_ref, lhigh_ref, y_ref, zlow_ref, zhigh_ref,
                 dlow_ref, dhigh_ref, k_out, n_out, stage_ref, sems):
-    fi, fj, fk = flags[0], flags[1], flags[2]
+    fi, fj, fk = scalars(flags_ref)
     last = ctrl - 1
     inner = ctrl - 2
     rows = lax.broadcasted_iota(jnp.int32, (ROWS, LANES), 0)
@@ -329,10 +353,9 @@
     values, slopes = spline_tables(quad // 2)
     wf_np, wb_np = plane_tables(values, slopes)
     wf, wb = jnp.asarray(wf_np), jnp.asarray(wb_np)
-    flags = orient.reshape(3)
+    flags = orient.reshape(1, 3)
     hbm = pl.BlockSpec(memory_space=pltpu.HBM)
     vmem = pl.BlockSpec(memory_space=pltpu.VMEM)
-    smem = pl.BlockSpec(memory_space=pltpu.SMEM)
     area = quad * quad
     nx, ny, nz = sizes
     face = 2 * ctrl * ctrl
@@ -363,13 +386,13 @@
     inputs = (flags, control_values, metric_diag, metric_off, mass_weight, wf, wb)
     bulk, xlow, xhigh, dlow, dhigh = call(
         functools.partial(body_kernel, values, slopes),
-        20,
+        24,
         10**9,
         out_shape=[sd(2, ctrl, vecs // LANES, ctrl * ROWS, LANES)] + [sd(8 * ctrl, vecs)] * 2 + [sd(4 * ctrl, vecs)] * 2,
         in_specs=[hbm] * 7,
         out_specs=[vmem] * 5,
         scratch_shapes=[
-            pltpu.SMEM((3,), jnp.int32),
+            pltpu.VMEM((1, 3), jnp.int32),
             pltpu.VMEM(control_values.shape, F32),
             pltpu.VMEM(metric_diag.shape, F32),
             pltpu.VMEM(metric_off.shape, F32),
@@ -378,10 +401,11 @@
             pltpu.VMEM(wb.shape, BF16),
             pltpu.SemaphoreType.DMA((ctrl,)),
             pltpu.SemaphoreType.DMA((6,)),
-            pltpu.VMEM((ctrl, 3 * area, vecs), F32),
             pltpu.VMEM((7, area, LANES), F32),
-            pltpu.VMEM((7 * quad, quad, LANES), F32),
-            pltpu.VMEM((ctrl, 4 * area, vecs), F32),
+            pltpu.VMEM((quad, 2, 3 * ROWS * ROWS, vecs), BF16),
+            pltpu.VMEM((quad, 4 * area, vecs), F32),
+            pltpu.VMEM((quad, 8 * area, vecs), BF16),
+            pltpu.VMEM((quad, 3 * ctrl * ROWS, vecs), F32),
         ],
     )(*(pltpu.with_memory_space_constraint(x, pltpu.HBM) for x in inputs))
     xlow_in = shifted(xhigh, ("px",), (nx,), (1,))
@@ -393,7 +417,7 @@
         8,
         10**8,
         out_shape=[sd(2 * face, vecs)] + [sd(face, vecs)] * 2,
-        in_specs=[smem] + [vmem] * 3,
+        in_specs=[vmem] + [vmem] * 3,
         out_specs=[vmem] * 3,
     )(flags, bulk, xlow_in, xhigh_in)
     zlow_in = shifted(zhigh, ("pz",), (nz,), (1,))
@@ -405,7 +429,7 @@
         8,
         10**7,
         out_shape=[sd(late, vecs)] * 2,
-        in_specs=[smem] + [vmem] * 3,
+        in_specs=[vmem] + [vmem] * 3,
         out_specs=[vmem] * 2,
     )(flags, bulk, dlow_in, dhigh_in)
     llow_in = shifted(lhigh, ("px",), (nx,), (1,))
@@ -416,7 +440,7 @@
             10,
             10**8,
             out_shape=[sd(*control_values.shape)] * 2,
-            in_specs=[smem] + [vmem] * 10,
+            in_specs=[vmem] + [vmem] * 10,
             out_specs=[hbm] * 2,
             scratch_shapes=[pltpu.VMEM((2, *control_values.shape), F32), pltpu.SemaphoreType.DMA((2, ctrl))],
         )(flags, bulk, xlow_in, xhigh_in, llow_in, lhigh_in, y_in, zlow_in, zhigh_in, dlow_in, dhigh_in)

time: 35.3 us -> 33.4 us (0.946)
  Pallas kernels: 10.3 us -> 7.87 us
  waiting for transfers between devices: 9.77 us -> 10.2 us
    pallas_call x4, Pallas kernels: 10.3 us -> 7.87 us  [run(): pl.pallas_call(kernel, compiler_params=pltpu.CompilerParams(vmem_limit_by...]
    ppermute x9, waiting for transfers between devices: 9.77 us -> 10.2 us  [shifted(): return lax.ppermute(x, axes, pairs)]
  transfers between devices with their start and end apart: 9 -> 9, of which waited for: 6 -> 7; matrix products, arithmetic and copies ran while one was open for 0% -> 0% of each run, Pallas kernels for 2% -> 0%
where the time goes in v1:
time: 33.4 us; the launch traced here: 33.2 us
  starting transfers between devices  14.5 us (43%)
  waiting for transfers between devices  10.2 us (31%)
  Pallas kernels  7.87 us (24%)
  between operations  0.67 us (2%)
    ppermute x9, starting transfers between devices, shifted(): return lax.ppermute(x, axes, pairs)  14.5 us
    ppermute x9, waiting for transfers between devices, shifted(): return lax.ppermute(x, axes, pairs)  10.2 us
    pallas_call x4, Pallas kernels, run(): pl.pallas_call(kernel, compiler_params=pltpu.CompilerParams(vmem_limit_by...  7.87 us
  transfers between devices with their start and end apart: 9, of which 7 were waited for; matrix products, arithmetic and copies ran while one was open for 0% of the time, Pallas kernels for 0%

profile of v1, /device:TPU:0, one launch (start us, length us, event | category | flops | bytes accessed | tf_op | source)
XLA Modules:
  0.0 33.2 jit_solution(11154466092478942963)
XLA Ops:
  0.6 0.0 copy-start
  0.6 6.0 %shard_map.86 = (f32[2,7,4,56,128]{4,3,2,1,0:T(8,128)S(1)}, f32[56,512]{1,0:T(8,128)S(1)}, f32[56,512]{1,0:T(8,128)S(1)}, f32[28,512]{1,0:T(8,128)S(1)}, f32[28,512]{1,0:T(8,128)S(1)}) custom-call(s32[1,3]{1,0:T(1,128)} %bitcast.1, f32[7,7,7,512]{3,2,1,0:T(8,128)} %u_in.1, f32[3,8,64]{2,1,0:T(8,128)} %diag_in.1, f32[3,8,64]{2,1,0:T(8,128)} %off_in.1, ...), custom_call_target="tpu_custom_call" | custom-call | flops 1000000000 | bytes 1000000 | tf_op jit(solution)/shard_map/pallas_call | solution.py:368
  6.7 0.5 %collective-permute-start = (f32[56,512]{1,0:T(8,128)S(1)}, f32[56,512]{1,0:T(8,128)S(1)}, u32[]{:S(2)}, u32[]{:S(2)}) collective-permute-start(f32[56,512]{1,0:T(8,128)S(1)} %get-tuple-element.13), channel_id=1, source_target_pairs={{0,8},{8,16},{16,24},{24,0},{1,9},{9,17},{17,25},{25,1},{2,10},{10... | collective-permute-start | bytes 344072 | tf_op jit(solution)/shard_map/ppermute | solution.py:347
  7.2 2.0 %collective-permute-start.1 = (f32[56,512]{1,0:T(8,128)S(1)}, f32[56,512]{1,0:T(8,128)S(1)}, u32[]{:S(2)}, u32[]{:S(2)}) collective-permute-start(f32[56,512]{1,0:T(8,128)S(1)} %get-tuple-element.14), channel_id=1, source_target_pairs={{0,24},{8,0},{16,8},{24,16},{1,25},{9,1},{17,9},{25,17},{2,26},{10... | collective-permute-start | bytes 344072 | tf_op jit(solution)/shard_map/ppermute | solution.py:347
  9.2 2.4 %collective-permute-done.xlow_ref = f32[56,512]{1,0:T(8,128)S(1)} collective-permute-done((f32[56,512]{1,0:T(8,128)S(1)}, f32[56,512]{1,0:T(8,128)S(1)}, u32[]{:S(2)}, u32[]{:S(2)}) %collective-permute-start) | collective-permute-done | bytes 114720 | tf_op jit(solution)/shard_map/ppermute | solution.py:347
  11.6 1.0 %collective-permute-done.1.xhigh_ref = f32[56,512]{1,0:T(8,128)S(1)} collective-permute-done((f32[56,512]{1,0:T(8,128)S(1)}, f32[56,512]{1,0:T(8,128)S(1)}, u32[]{:S(2)}, u32[]{:S(2)}) %collective-permute-start.1) | collective-permute-done | bytes 114720 | tf_op jit(solution)/shard_map/ppermute | solution.py:347
  12.7 0.0 copy-done
  12.7 0.3 shard_map.88
  13.0 1.6 %collective-permute-start.6 = (f32[196,512]{1,0:T(8,128)S(1)}, f32[196,512]{1,0:T(8,128)S(1)}, u32[]{:S(2)}, u32[]{:S(2)}) collective-permute-start(f32[196,512]{1,0:T(8,128)S(1)} %get-tuple-element.19), channel_id=1, source_target_pairs={{0,4},{4,0},{1,5},{5,1},{2,6},{6,2},{3,7},{7,3},{8,12},{12,8},{9,1... | collective-permute-start | bytes 1204232 | tf_op jit(solution)/shard_map/ppermute | solution.py:347
  14.6 1.5 %collective-permute-start.2 = (f32[28,512]{1,0:T(8,128)S(1)}, f32[28,512]{1,0:T(8,128)S(1)}, u32[]{:S(2)}, u32[]{:S(2)}) collective-permute-start(f32[28,512]{1,0:T(8,128)S(1)} %get-tuple-element.15), channel_id=1, source_target_pairs={{0,5},{1,6},{2,7},{3,4},{4,1},{5,2},{6,3},{7,0},{8,13},{9,14},{10,... | collective-permute-start | bytes 172040 | tf_op jit(solution)/shard_map/ppermute | solution.py:347
  16.1 3.2 %collective-permute-start.3 = (f32[28,512]{1,0:T(8,128)S(1)}, f32[28,512]{1,0:T(8,128)S(1)}, u32[]{:S(2)}, u32[]{:S(2)}) collective-permute-start(f32[28,512]{1,0:T(8,128)S(1)} %get-tuple-element.16), channel_id=1, source_target_pairs={{0,7},{1,4},{2,5},{3,6},{4,3},{5,0},{6,1},{7,2},{8,15},{9,12},{10,... | collective-permute-start | bytes 172040 | tf_op jit(solution)/shard_map/ppermute | solution.py:347
  19.3 0.0 collective-permute-start.7
  19.3 3.8 %collective-permute-start.8 = (f32[98,512]{1,0:T(8,128)S(1)}, f32[98,512]{1,0:T(8,128)S(1)}, u32[]{:S(2)}, u32[]{:S(2)}) collective-permute-start(f32[98,512]{1,0:T(8,128)S(1)} %get-tuple-element.21), channel_id=1, source_target_pairs={{0,3},{1,0},{2,1},{3,2},{4,7},{5,4},{6,5},{7,6},{8,11},{9,8},{10,9... | collective-permute-start | bytes 602120 | tf_op jit(solution)/shard_map/ppermute | solution.py:347
  23.1 0.0 collective-permute-done.2.dlow_ref
  23.1 0.3 collective-permute-done.3.dhigh_ref
  23.4 0.1 shard_map.87
  23.5 0.1 collective-permute-start.4
  23.6 1.7 %collective-permute-start.5 = (f32[78,512]{1,0:T(8,128)S(1)}, f32[78,512]{1,0:T(8,128)S(1)}, u32[]{:S(2)}, u32[]{:S(2)}) collective-permute-start(f32[78,512]{1,0:T(8,128)S(1)} %get-tuple-element.18), channel_id=1, source_target_pairs={{0,24},{8,0},{16,8},{24,16},{1,25},{9,1},{17,9},{25,17},{2,26},{10... | collective-permute-start | bytes 479240 | tf_op jit(solution)/shard_map/ppermute | solution.py:347
  25.3 3.0 %collective-permute-done.4.llow_ref = f32[78,512]{1,0:T(8,128)S(1)} collective-permute-done((f32[78,512]{1,0:T(8,128)S(1)}, f32[78,512]{1,0:T(8,128)S(1)}, u32[]{:S(2)}, u32[]{:S(2)}) %collective-permute-start.4) | collective-permute-done | bytes 159776 | tf_op jit(solution)/shard_map/ppermute | solution.py:347
  28.3 0.7 %collective-permute-done.5.lhigh_ref = f32[78,512]{1,0:T(8,128)S(1)} collective-permute-done((f32[78,512]{1,0:T(8,128)S(1)}, f32[78,512]{1,0:T(8,128)S(1)}, u32[]{:S(2)}, u32[]{:S(2)}) %collective-permute-start.5) | collective-permute-done | bytes 159776 | tf_op jit(solution)/shard_map/ppermute | solution.py:347
  29.0 0.2 collective-permute-done.7.zlow_ref
  29.3 2.6 %collective-permute-done.8.zhigh_ref = f32[98,512]{1,0:T(8,128)S(1)} collective-permute-done((f32[98,512]{1,0:T(8,128)S(1)}, f32[98,512]{1,0:T(8,128)S(1)}, u32[]{:S(2)}, u32[]{:S(2)}) %collective-permute-start.8) | collective-permute-done | bytes 200736 | tf_op jit(solution)/shard_map/ppermute | solution.py:347
  31.8 0.0 collective-permute-done.6.y_ref
  31.8 1.4 %shard_map.89 = (f32[7,7,7,512]{3,2,1,0:T(8,128)}, f32[7,7,7,512]{3,2,1,0:T(8,128)}) custom-call(s32[1,3]{1,0:T(1,128)S(1)} %bitcast.4, f32[2,7,4,56,128]{4,3,2,1,0:T(8,128)S(1)} %get-tuple-element.12.bulk_ref, f32[56,512]{1,0:T(8,128)S(1)} %collective-permute-done.xlow_ref, f32[56,512]{1,0:T(8,128)S(1)} %collective-permute-done.1.xhigh_ref, ...), custom_call_target="tpu_custom_call" | custom-call | flops 100000000 | bytes 1000000 | tf_op jit(solution)/shard_map/pallas_call | solution.py:368
Async XLA Ops:
  0.6 12.0 %copy-start = (s32[1,1,1,3]{3,2,1,0:T(1,128)S(1)}, s32[1,1,1,3]{3,2,1,0:T(1,128)}, u32[]{:S(2)}) copy-start(s32[1,1,1,3]{3,2,1,0:T(1,128)} %param.11) | copy-start | bytes 40
  6.7 4.9 %collective-permute-start = (f32[56,512]{1,0:T(8,128)S(1)}, f32[56,512]{1,0:T(8,128)S(1)}, u32[]{:S(2)}, u32[]{:S(2)}) collective-permute-start(f32[56,512]{1,0:T(8,128)S(1)} %get-tuple-element.13), channel_id=1, source_target_pairs={{0,8},{8,16},{16,24},{24,0},{1,9},{9,17},{17,25},{25,1},{2,10},{10... | collective-permute-start | bytes 344072 | tf_op jit(solution)/shard_map/ppermute | solution.py:347
  7.2 5.4 %collective-permute-start.1 = (f32[56,512]{1,0:T(8,128)S(1)}, f32[56,512]{1,0:T(8,128)S(1)}, u32[]{:S(2)}, u32[]{:S(2)}) collective-permute-start(f32[56,512]{1,0:T(8,128)S(1)} %get-tuple-element.14), channel_id=1, source_target_pairs={{0,24},{8,0},{16,8},{24,16},{1,25},{9,1},{17,9},{25,17},{2,26},{10... | collective-permute-start | bytes 344072 | tf_op jit(solution)/shard_map/ppermute | solution.py:347
  13.0 18.9 %collective-permute-start.6 = (f32[196,512]{1,0:T(8,128)S(1)}, f32[196,512]{1,0:T(8,128)S(1)}, u32[]{:S(2)}, u32[]{:S(2)}) collective-permute-start(f32[196,512]{1,0:T(8,128)S(1)} %get-tuple-element.19), channel_id=1, source_target_pairs={{0,4},{4,0},{1,5},{5,1},{2,6},{6,2},{3,7},{7,3},{8,12},{12,8},{9,1... | collective-permute-start | bytes 1204232 | tf_op jit(solution)/shard_map/ppermute | solution.py:347
  14.6 8.6 %collective-permute-start.2 = (f32[28,512]{1,0:T(8,128)S(1)}, f32[28,512]{1,0:T(8,128)S(1)}, u32[]{:S(2)}, u32[]{:S(2)}) collective-permute-start(f32[28,512]{1,0:T(8,128)S(1)} %get-tuple-element.15), channel_id=1, source_target_pairs={{0,5},{1,6},{2,7},{3,4},{4,1},{5,2},{6,3},{7,0},{8,13},{9,14},{10,... | collective-permute-start | bytes 172040 | tf_op jit(solution)/shard_map/ppermute | solution.py:347
  16.1 7.3 %collective-permute-start.3 = (f32[28,512]{1,0:T(8,128)S(1)}, f32[28,512]{1,0:T(8,128)S(1)}, u32[]{:S(2)}, u32[]{:S(2)}) collective-permute-start(f32[28,512]{1,0:T(8,128)S(1)} %get-tuple-element.16), channel_id=1, source_target_pairs={{0,7},{1,4},{2,5},{3,6},{4,3},{5,0},{6,1},{7,2},{8,15},{9,12},{10,... | collective-permute-start | bytes 172040 | tf_op jit(solution)/shard_map/ppermute | solution.py:347
  19.3 10.0 %collective-permute-start.7 = (f32[98,512]{1,0:T(8,128)S(1)}, f32[98,512]{1,0:T(8,128)S(1)}, u32[]{:S(2)}, u32[]{:S(2)}) collective-permute-start(f32[98,512]{1,0:T(8,128)S(1)} %get-tuple-element.20), channel_id=1, source_target_pairs={{0,1},{1,2},{2,3},{3,0},{4,5},{5,6},{6,7},{7,4},{8,9},{9,10},{10,1... | collective-permute-start | bytes 602120 | tf_op jit(solution)/shard_map/ppermute | solution.py:347
  19.3 12.5 %collective-permute-start.8 = (f32[98,512]{1,0:T(8,128)S(1)}, f32[98,512]{1,0:T(8,128)S(1)}, u32[]{:S(2)}, u32[]{:S(2)}) collective-permute-start(f32[98,512]{1,0:T(8,128)S(1)} %get-tuple-element.21), channel_id=1, source_target_pairs={{0,3},{1,0},{2,1},{3,2},{4,7},{5,4},{6,5},{7,6},{8,11},{9,8},{10,9... | collective-permute-start | bytes 602120 | tf_op jit(solution)/shard_map/ppermute | solution.py:347
  23.5 4.8 %collective-permute-start.4 = (f32[78,512]{1,0:T(8,128)S(1)}, f32[78,512]{1,0:T(8,128)S(1)}, u32[]{:S(2)}, u32[]{:S(2)}) collective-permute-start(f32[78,512]{1,0:T(8,128)S(1)} %get-tuple-element.17), channel_id=1, source_target_pairs={{0,8},{8,16},{16,24},{24,0},{1,9},{9,17},{17,25},{25,1},{2,10},{10... | collective-permute-start | bytes 479240 | tf_op jit(solution)/shard_map/ppermute | solution.py:347
  23.6 5.5 %collective-permute-start.5 = (f32[78,512]{1,0:T(8,128)S(1)}, f32[78,512]{1,0:T(8,128)S(1)}, u32[]{:S(2)}, u32[]{:S(2)}) collective-permute-start(f32[78,512]{1,0:T(8,128)S(1)} %get-tuple-element.18), channel_id=1, source_target_pairs={{0,24},{8,0},{16,8},{24,16},{1,25},{9,1},{17,9},{25,17},{2,26},{10... | collective-permute-start | bytes 479240 | tf_op jit(solution)/shard_map/ppermute | solution.py:347

commit v2 on v1

--- a/solution.py
+++ b/solution.py
@@ -241,7 +241,7 @@
                 x_ref[pl.ds((line * 2 + field) * ctrl, ctrl), cols] = z_line(bulk_ref, field, here, lane, k, flags, ctrl)
         for i, (side, j), (k, d_ref) in itertools.product(range(ctrl), ((0, 0), (1, last)), ((0, dlow_ref), (last, dhigh_ref))):
             row = at(j, fj, ctrl) * ROWS + at(k, fk, ctrl)
-            d_ref[pl.ds((side * 2 + field) * ctrl + i, 1), cols] = bulk_ref[field, at(i, fi, ctrl), lane, pl.ds(row, 1), :]
+            d_ref[pl.ds(((side * lanes + lane) * 2 + field) * ctrl + i, 1), :] = bulk_ref[field, at(i, fi, ctrl), lane, pl.ds(row, 1), :]
 
 
 def y_line(bulk_ref, field, here, lane, j, flags, ctrl):
@@ -258,7 +258,8 @@
 def pack_kernel(ctrl, flags_ref, bulk_ref, xlow_ref, xhigh_ref, y_ref, zlow_ref, zhigh_ref):
     flags = scalars(flags_ref)
     last = ctrl - 1
-    for field, i, lane in np.ndindex(2, ctrl, bulk_ref.shape[2]):
+    lanes = bulk_ref.shape[2]
+    for field, i, lane in np.ndindex(2, ctrl, lanes):
         here = at(i, flags[0], ctrl)
         cols = pl.ds(lane * LANES, LANES)
         x_ref = xlow_ref if i == 0 else xhigh_ref if i == last else None
@@ -268,27 +269,28 @@
 
         for side, j in ((0, 0), (1, last)):
             block = y_line(bulk_ref, field, here, lane, j, flags, ctrl)
-            y_ref[pl.ds(((side * 2 + field) * ctrl + i) * ctrl, ctrl), cols] = summed(block, side)
+            y_ref[pl.ds((((side * lanes + lane) * 2 + field) * ctrl + i) * ctrl, ctrl), :] = summed(block, side)
         for side, k, z_ref in ((0, 0, zlow_ref), (1, last, zhigh_ref)):
             block = z_line(bulk_ref, field, here, lane, k, flags, ctrl)
-            z_ref[pl.ds((field * ctrl + i) * ctrl, ctrl), cols] = summed(block, 2 + side)
+            z_ref[pl.ds(((lane * 2 + field) * ctrl + i) * ctrl, ctrl), :] = summed(block, 2 + side)
 
 
 def late_kernel(ctrl, flags_ref, bulk_ref, dlow_ref, dhigh_ref, low_ref, high_ref):
     flags = scalars(flags_ref)
     last = ctrl - 1
     inner = ctrl - 2
+    lanes = bulk_ref.shape[2]
+    count = 2 * inner * ctrl + 8
     for i, out_ref in ((0, low_ref), (last, high_ref)):
         here = at(i, flags[0], ctrl)
-        for field, lane in np.ndindex(2, bulk_ref.shape[2]):
-            cols = pl.ds(lane * LANES, LANES)
+        for lane, field in np.ndindex(lanes, 2):
             for j in range(1, last):
                 block = y_line(bulk_ref, field, here, lane, j, flags, ctrl)
-                out_ref[pl.ds((field * inner + j - 1) * ctrl, ctrl), cols] = block
-        for end, d_ref in enumerate((dlow_ref, dhigh_ref)):
-            for side, field in np.ndindex(2, 2):
-                row = 2 * inner * ctrl + (end * 2 + side) * 2 + field
-                out_ref[pl.ds(row, 1), :] = d_ref[pl.ds((side * 2 + field) * ctrl + i, 1), :]
+                out_ref[pl.ds(lane * count + (field * inner + j - 1) * ctrl, ctrl), :] = block
+            for end, d_ref in enumerate((dlow_ref, dhigh_ref)):
+                for side in range(2):
+                    row = lane * count + 2 * inner * ctrl + (end * 2 + side) * 2 + field
+                    out_ref[pl.ds(row, 1), :] = d_ref[pl.ds(((side * lanes + lane) * 2 + field) * ctrl + i, 1), :]
 
 
 def join_kernel(ctrl, flags_ref, bulk_ref, xlow_ref, xhigh_ref, llow_ref, lhigh_ref, y_ref, zlow_ref, zhigh_ref,
@@ -299,6 +301,8 @@
     rows = lax.broadcasted_iota(jnp.int32, (ROWS, LANES), 0)
     at_low, at_high = rows == at(0, fk, ctrl), rows == at(last, fk, ctrl)
     pad = jnp.zeros((ROWS - ctrl, LANES), F32)
+    lanes = bulk_ref.shape[2]
+    count = 2 * inner * ctrl + 8
     copies = []
 
     def spread(row):
@@ -315,20 +319,20 @@
             extra = []
             if x_ref is not None:
                 if rim is None:
-                    extra.append(l_ref[pl.ds((field * inner + j - 1) * ctrl, ctrl), cols])
+                    extra.append(l_ref[pl.ds(lane * count + (field * inner + j - 1) * ctrl, ctrl), :])
                 else:
                     extra.append(x_ref[pl.ds(((1 - rim) * 2 + field) * ctrl, ctrl), cols])
             if rim is not None:
-                extra.append(y_ref[pl.ds(((rim * 2 + field) * ctrl + i) * ctrl, ctrl), cols])
+                extra.append(y_ref[pl.ds((((rim * lanes + lane) * 2 + field) * ctrl + i) * ctrl, ctrl), :])
             if extra:
                 block = block + turned(jnp.concatenate([sum(extra[1:], extra[0]), pad], axis=0), fk, ctrl)
             ends = []
             for end, (z_ref, d_ref) in enumerate(((zlow_ref, dlow_ref), (zhigh_ref, dhigh_ref))):
-                row = z_ref[pl.ds((field * ctrl + i) * ctrl + j, 1), cols]
+                row = z_ref[pl.ds(((lane * 2 + field) * ctrl + i) * ctrl + j, 1), :]
                 if rim is not None:
-                    row = row + d_ref[pl.ds((rim * 2 + field) * ctrl + i, 1), cols]
+                    row = row + d_ref[pl.ds(((rim * lanes + lane) * 2 + field) * ctrl + i, 1), :]
                     if l_ref is not None:
-                        row = row + l_ref[pl.ds(2 * inner * ctrl + (end * 2 + rim) * 2 + field, 1), cols]
+                        row = row + l_ref[pl.ds(lane * count + 2 * inner * ctrl + (end * 2 + rim) * 2 + field, 1), :]
                 ends.append(spread(row))
             block = block + jnp.where(at_low, ends[0], jnp.where(at_high, ends[1], 0.0))
             stage_ref[field, i, there, :, cols] = block[0:ctrl]
@@ -359,6 +363,7 @@
     area = quad * quad
     nx, ny, nz = sizes
     face = 2 * ctrl * ctrl
+    lanes = vecs // LANES
 
     def sd(*shape):
         return jax.ShapeDtypeStruct(shape, F32)
@@ -388,7 +393,7 @@
         functools.partial(body_kernel, values, slopes),
         24,
         10**9,
-        out_shape=[sd(2, ctrl, vecs // LANES, ctrl * ROWS, LANES)] + [sd(8 * ctrl, vecs)] * 2 + [sd(4 * ctrl, vecs)] * 2,
+        out_shape=[sd(2, ctrl, vecs // LANES, ctrl * ROWS, LANES)] + [sd(8 * ctrl, vecs)] * 2 + [sd(4 * ctrl * lanes, LANES)] * 2,
         in_specs=[hbm] * 7,
         out_specs=[vmem] * 5,
         scratch_shapes=[
@@ -416,7 +421,7 @@
         functools.partial(pack_kernel, ctrl),
         8,
         10**8,
-        out_shape=[sd(2 * face, vecs)] + [sd(face, vecs)] * 2,
+        out_shape=[sd(2 * face * lanes, LANES)] + [sd(face * lanes, LANES)] * 2,
         in_specs=[vmem] + [vmem] * 3,
         out_specs=[vmem] * 3,
     )(flags, bulk, xlow_in, xhigh_in)
@@ -428,7 +433,7 @@
         functools.partial(late_kernel, ctrl),
         8,
         10**7,
-        out_shape=[sd(late, vecs)] * 2,
+        out_shape=[sd(late * lanes, LANES)] * 2,
         in_specs=[vmem] + [vmem] * 3,
         out_specs=[vmem] * 2,
     )(flags, bulk, dlow_in, dhigh_in)

time: 33.4 us -> 32.5 us (0.973)
  waiting for transfers between devices: 10.2 us -> 9.42 us
    ppermute x9, waiting for transfers between devices: 10.2 us -> 9.42 us  [shifted(): return lax.ppermute(x, axes, pairs)]
  transfers between devices with their start and end apart: 9 -> 9, of which waited for: 7 -> 6; matrix products, arithmetic and copies ran while one was open for 0% -> 0% of each run, Pallas kernels for 0% -> 0%
where the time goes in v2:
time: 32.5 us; the launch traced here: 32.4 us
  starting transfers between devices  14.5 us (45%)
  waiting for transfers between devices  9.42 us (29%)
  Pallas kernels  7.85 us (24%)
  between operations  0.67 us (2%)
    ppermute x9, starting transfers between devices, shifted(): return lax.ppermute(x, axes, pairs)  14.5 us
    ppermute x9, waiting for transfers between devices, shifted(): return lax.ppermute(x, axes, pairs)  9.42 us
    pallas_call x4, Pallas kernels, run(): pl.pallas_call(kernel, compiler_params=pltpu.CompilerParams(vmem_limit_by...  7.85 us
  transfers between devices with their start and end apart: 9, of which 6 were waited for; matrix products, arithmetic and copies ran while one was open for 0% of the time, Pallas kernels for 0%

profile of v2, /device:TPU:0, one launch (start us, length us, event | category | flops | bytes accessed | tf_op | source)
XLA Modules:
  0.0 32.4 jit_solution(15656394848567176503)
XLA Ops:
  0.6 0.0 copy-start
  0.6 6.0 %shard_map.86 = (f32[2,7,4,56,128]{4,3,2,1,0:T(8,128)S(1)}, f32[56,512]{1,0:T(8,128)S(1)}, f32[56,512]{1,0:T(8,128)S(1)}, f32[112,128]{1,0:T(8,128)S(1)}, f32[112,128]{1,0:T(8,128)S(1)}) custom-call(s32[1,3]{1,0:T(1,128)} %bitcast.1, f32[7,7,7,512]{3,2,1,0:T(8,128)} %u_in.1, f32[3,8,64]{2,1,0:T(8,128)} %diag_in.1, f32[3,8,64]{2,1,0:T(8,128)} %off_in.1, ...), custom_call_target="tpu_custom_call" | custom-call | flops 1000000000 | bytes 1000000 | tf_op jit(solution)/shard_map/pallas_call | solution.py:373
  6.7 0.5 %collective-permute-start = (f32[56,512]{1,0:T(8,128)S(1)}, f32[56,512]{1,0:T(8,128)S(1)}, u32[]{:S(2)}, u32[]{:S(2)}) collective-permute-start(f32[56,512]{1,0:T(8,128)S(1)} %get-tuple-element.13), channel_id=1, source_target_pairs={{0,8},{8,16},{16,24},{24,0},{1,9},{9,17},{17,25},{25,1},{2,10},{10... | collective-permute-start | bytes 344072 | tf_op jit(solution)/shard_map/ppermute | solution.py:351
  7.2 2.0 %collective-permute-start.1 = (f32[56,512]{1,0:T(8,128)S(1)}, f32[56,512]{1,0:T(8,128)S(1)}, u32[]{:S(2)}, u32[]{:S(2)}) collective-permute-start(f32[56,512]{1,0:T(8,128)S(1)} %get-tuple-element.14), channel_id=1, source_target_pairs={{0,24},{8,0},{16,8},{24,16},{1,25},{9,1},{17,9},{25,17},{2,26},{10... | collective-permute-start | bytes 344072 | tf_op jit(solution)/shard_map/ppermute | solution.py:351
  9.2 2.4 %collective-permute-done.xlow_ref = f32[56,512]{1,0:T(8,128)S(1)} collective-permute-done((f32[56,512]{1,0:T(8,128)S(1)}, f32[56,512]{1,0:T(8,128)S(1)}, u32[]{:S(2)}, u32[]{:S(2)}) %collective-permute-start) | collective-permute-done | bytes 114720 | tf_op jit(solution)/shard_map/ppermute | solution.py:351
  11.6 1.0 %collective-permute-done.1.xhigh_ref = f32[56,512]{1,0:T(8,128)S(1)} collective-permute-done((f32[56,512]{1,0:T(8,128)S(1)}, f32[56,512]{1,0:T(8,128)S(1)}, u32[]{:S(2)}, u32[]{:S(2)}) %collective-permute-start.1) | collective-permute-done | bytes 114720 | tf_op jit(solution)/shard_map/ppermute | solution.py:351
  12.7 0.0 copy-done
  12.7 0.3 shard_map.88
  12.9 1.6 %collective-permute-start.6 = (f32[784,128]{1,0:T(8,128)S(1)}, f32[784,128]{1,0:T(8,128)S(1)}, u32[]{:S(2)}, u32[]{:S(2)}) collective-permute-start(f32[784,128]{1,0:T(8,128)S(1)} %get-tuple-element.19), channel_id=1, source_target_pairs={{0,4},{4,0},{1,5},{5,1},{2,6},{6,2},{3,7},{7,3},{8,12},{12,8},{9,1... | collective-permute-start | bytes 1204232 | tf_op jit(solution)/shard_map/ppermute | solution.py:351
  14.5 1.5 %collective-permute-start.2 = (f32[112,128]{1,0:T(8,128)S(1)}, f32[112,128]{1,0:T(8,128)S(1)}, u32[]{:S(2)}, u32[]{:S(2)}) collective-permute-start(f32[112,128]{1,0:T(8,128)S(1)} %get-tuple-element.15), channel_id=1, source_target_pairs={{0,5},{1,6},{2,7},{3,4},{4,1},{5,2},{6,3},{7,0},{8,13},{9,14},{10,... | collective-permute-start | bytes 172040 | tf_op jit(solution)/shard_map/ppermute | solution.py:351
  16.0 3.2 %collective-permute-start.3 = (f32[112,128]{1,0:T(8,128)S(1)}, f32[112,128]{1,0:T(8,128)S(1)}, u32[]{:S(2)}, u32[]{:S(2)}) collective-permute-start(f32[112,128]{1,0:T(8,128)S(1)} %get-tuple-element.16), channel_id=1, source_target_pairs={{0,7},{1,4},{2,5},{3,6},{4,3},{5,0},{6,1},{7,2},{8,15},{9,12},{10,... | collective-permute-start | bytes 172040 | tf_op jit(solution)/shard_map/ppermute | solution.py:351
  19.3 0.0 collective-permute-start.7
  19.3 3.8 %collective-permute-start.8 = (f32[392,128]{1,0:T(8,128)S(1)}, f32[392,128]{1,0:T(8,128)S(1)}, u32[]{:S(2)}, u32[]{:S(2)}) collective-permute-start(f32[392,128]{1,0:T(8,128)S(1)} %get-tuple-element.21), channel_id=1, source_target_pairs={{0,3},{1,0},{2,1},{3,2},{4,7},{5,4},{6,5},{7,6},{8,11},{9,8},{10,9... | collective-permute-start | bytes 602120 | tf_op jit(solution)/shard_map/ppermute | solution.py:351
  23.1 0.0 collective-permute-done.2.dlow_ref
  23.1 0.0 collective-permute-done.3.dhigh_ref
  23.1 0.1 shard_map.87
  23.2 0.1 collective-permute-start.4
  23.3 1.7 %collective-permute-start.5 = (f32[312,128]{1,0:T(8,128)S(1)}, f32[312,128]{1,0:T(8,128)S(1)}, u32[]{:S(2)}, u32[]{:S(2)}) collective-permute-start(f32[312,128]{1,0:T(8,128)S(1)} %get-tuple-element.18), channel_id=1, source_target_pairs={{0,24},{8,0},{16,8},{24,16},{1,25},{9,1},{17,9},{25,17},{2,26},{10... | collective-permute-start | bytes 479240 | tf_op jit(solution)/shard_map/ppermute | solution.py:351
  25.0 3.0 %collective-permute-done.4.llow_ref = f32[312,128]{1,0:T(8,128)S(1)} collective-permute-done((f32[312,128]{1,0:T(8,128)S(1)}, f32[312,128]{1,0:T(8,128)S(1)}, u32[]{:S(2)}, u32[]{:S(2)}) %collective-permute-start.4) | collective-permute-done | bytes 159776 | tf_op jit(solution)/shard_map/ppermute | solution.py:351
  28.0 0.9 %collective-permute-done.5.lhigh_ref = f32[312,128]{1,0:T(8,128)S(1)} collective-permute-done((f32[312,128]{1,0:T(8,128)S(1)}, f32[312,128]{1,0:T(8,128)S(1)}, u32[]{:S(2)}, u32[]{:S(2)}) %collective-permute-start.5) | collective-permute-done | bytes 159776 | tf_op jit(solution)/shard_map/ppermute | solution.py:351
  28.9 0.1 collective-permute-done.7.zlow_ref
  29.0 2.0 %collective-permute-done.8.zhigh_ref = f32[392,128]{1,0:T(8,128)S(1)} collective-permute-done((f32[392,128]{1,0:T(8,128)S(1)}, f32[392,128]{1,0:T(8,128)S(1)}, u32[]{:S(2)}, u32[]{:S(2)}) %collective-permute-start.8) | collective-permute-done | bytes 200736 | tf_op jit(solution)/shard_map/ppermute | solution.py:351
  31.0 0.0 collective-permute-done.6.y_ref
  31.0 1.4 %shard_map.89 = (f32[7,7,7,512]{3,2,1,0:T(8,128)}, f32[7,7,7,512]{3,2,1,0:T(8,128)}) custom-call(s32[1,3]{1,0:T(1,128)S(1)} %bitcast.4, f32[2,7,4,56,128]{4,3,2,1,0:T(8,128)S(1)} %get-tuple-element.12.bulk_ref, f32[56,512]{1,0:T(8,128)S(1)} %collective-permute-done.xlow_ref, f32[56,512]{1,0:T(8,128)S(1)} %collective-permute-done.1.xhigh_ref, ...), custom_call_target="tpu_custom_call" | custom-call | flops 100000000 | bytes 1000000 | tf_op jit(solution)/shard_map/pallas_call | solution.py:373
Async XLA Ops:
  0.6 12.0 %copy-start = (s32[1,1,1,3]{3,2,1,0:T(1,128)S(1)}, s32[1,1,1,3]{3,2,1,0:T(1,128)}, u32[]{:S(2)}) copy-start(s32[1,1,1,3]{3,2,1,0:T(1,128)} %param.11) | copy-start | bytes 40
  6.7 4.9 %collective-permute-start = (f32[56,512]{1,0:T(8,128)S(1)}, f32[56,512]{1,0:T(8,128)S(1)}, u32[]{:S(2)}, u32[]{:S(2)}) collective-permute-start(f32[56,512]{1,0:T(8,128)S(1)} %get-tuple-element.13), channel_id=1, source_target_pairs={{0,8},{8,16},{16,24},{24,0},{1,9},{9,17},{17,25},{25,1},{2,10},{10... | collective-permute-start | bytes 344072 | tf_op jit(solution)/shard_map/ppermute | solution.py:351
  7.2 5.4 %collective-permute-start.1 = (f32[56,512]{1,0:T(8,128)S(1)}, f32[56,512]{1,0:T(8,128)S(1)}, u32[]{:S(2)}, u32[]{:S(2)}) collective-permute-start(f32[56,512]{1,0:T(8,128)S(1)} %get-tuple-element.14), channel_id=1, source_target_pairs={{0,24},{8,0},{16,8},{24,16},{1,25},{9,1},{17,9},{25,17},{2,26},{10... | collective-permute-start | bytes 344072 | tf_op jit(solution)/shard_map/ppermute | solution.py:351
  12.9 18.1 %collective-permute-start.6 = (f32[784,128]{1,0:T(8,128)S(1)}, f32[784,128]{1,0:T(8,128)S(1)}, u32[]{:S(2)}, u32[]{:S(2)}) collective-permute-start(f32[784,128]{1,0:T(8,128)S(1)} %get-tuple-element.19), channel_id=1, source_target_pairs={{0,4},{4,0},{1,5},{5,1},{2,6},{6,2},{3,7},{7,3},{8,12},{12,8},{9,1... | collective-permute-start | bytes 1204232 | tf_op jit(solution)/shard_map/ppermute | solution.py:351
  14.5 8.6 %collective-permute-start.2 = (f32[112,128]{1,0:T(8,128)S(1)}, f32[112,128]{1,0:T(8,128)S(1)}, u32[]{:S(2)}, u32[]{:S(2)}) collective-permute-start(f32[112,128]{1,0:T(8,128)S(1)} %get-tuple-element.15), channel_id=1, source_target_pairs={{0,5},{1,6},{2,7},{3,4},{4,1},{5,2},{6,3},{7,0},{8,13},{9,14},{10,... | collective-permute-start | bytes 172040 | tf_op jit(solution)/shard_map/ppermute | solution.py:351
  16.0 7.1 %collective-permute-start.3 = (f32[112,128]{1,0:T(8,128)S(1)}, f32[112,128]{1,0:T(8,128)S(1)}, u32[]{:S(2)}, u32[]{:S(2)}) collective-permute-start(f32[112,128]{1,0:T(8,128)S(1)} %get-tuple-element.16), channel_id=1, source_target_pairs={{0,7},{1,4},{2,5},{3,6},{4,3},{5,0},{6,1},{7,2},{8,15},{9,12},{10,... | collective-permute-start | bytes 172040 | tf_op jit(solution)/shard_map/ppermute | solution.py:351
  19.3 9.7 %collective-permute-start.7 = (f32[392,128]{1,0:T(8,128)S(1)}, f32[392,128]{1,0:T(8,128)S(1)}, u32[]{:S(2)}, u32[]{:S(2)}) collective-permute-start(f32[392,128]{1,0:T(8,128)S(1)} %get-tuple-element.20), channel_id=1, source_target_pairs={{0,1},{1,2},{2,3},{3,0},{4,5},{5,6},{6,7},{7,4},{8,9},{9,10},{10,1... | collective-permute-start | bytes 602120 | tf_op jit(solution)/shard_map/ppermute | solution.py:351
  19.3 11.7 %collective-permute-start.8 = (f32[392,128]{1,0:T(8,128)S(1)}, f32[392,128]{1,0:T(8,128)S(1)}, u32[]{:S(2)}, u32[]{:S(2)}) collective-permute-start(f32[392,128]{1,0:T(8,128)S(1)} %get-tuple-element.21), channel_id=1, source_target_pairs={{0,3},{1,0},{2,1},{3,2},{4,7},{5,4},{6,5},{7,6},{8,11},{9,8},{10,9... | collective-permute-start | bytes 602120 | tf_op jit(solution)/shard_map/ppermute | solution.py:351
  23.2 4.8 %collective-permute-start.4 = (f32[312,128]{1,0:T(8,128)S(1)}, f32[312,128]{1,0:T(8,128)S(1)}, u32[]{:S(2)}, u32[]{:S(2)}) collective-permute-start(f32[312,128]{1,0:T(8,128)S(1)} %get-tuple-element.17), channel_id=1, source_target_pairs={{0,8},{8,16},{16,24},{24,0},{1,9},{9,17},{17,25},{25,1},{2,10},{10... | collective-permute-start | bytes 479240 | tf_op jit(solution)/shard_map/ppermute | solution.py:351
  23.3 5.6 %collective-permute-start.5 = (f32[312,128]{1,0:T(8,128)S(1)}, f32[312,128]{1,0:T(8,128)S(1)}, u32[]{:S(2)}, u32[]{:S(2)}) collective-permute-start(f32[312,128]{1,0:T(8,128)S(1)} %get-tuple-element.18), channel_id=1, source_target_pairs={{0,24},{8,0},{16,8},{24,16},{1,25},{9,1},{17,9},{25,17},{2,26},{10... | collective-permute-start | bytes 479240 | tf_op jit(solution)/shard_map/ppermute | solution.py:351

commit v3 on v2

--- a/solution.py
+++ b/solution.py
@@ -212,14 +212,18 @@
         )
     ]
     planes = [pltpu.make_async_copy(u_in.at[i], u_ref.at[i], u_sems.at[i]) for i in range(ctrl)]
-    for copy in small[1:4] + planes + small[:1] + small[4:]:
+    for copy in small[:4] + planes + small[4:]:
         copy.start()
     for copy in small[1:4]:
         copy.wait()
     metric_stage(diag_ref, off_ref, weight_ref, t_ref)
-    for copy in planes + small[:1] + small[4:]:
+    needed = max(i for i in range(ctrl) if values[:2, i].any() or slopes[:2, i].any()) + 1
+    for copy in small[:1] + planes[:needed]:
         copy.wait()
     for step in range(quad + 2):
+        if step == 2:
+            for copy in planes[needed:] + small[4:]:
+                copy.wait()
         if step < quad:
             operand_stage(step, u_ref, v_ref, values, slopes)
             gradient_stage(step, v_ref, wf_ref, g_ref)

time: 32.5 us -> 32.3 us (level)
  no operation moved by 1% of the time
where the time goes in v3:
time: 32.3 us; the launch traced here: 32.1 us
  starting transfers between devices  14.4 us (45%)
  waiting for transfers between devices  9.42 us (29%)
  Pallas kernels  7.59 us (23%)
  between operations  0.67 us (2%)
    ppermute x9, starting transfers between devices, shifted(): return lax.ppermute(x, axes, pairs)  14.4 us
    ppermute x9, waiting for transfers between devices, shifted(): return lax.ppermute(x, axes, pairs)  9.42 us
    pallas_call x4, Pallas kernels, run(): pl.pallas_call(kernel, compiler_params=pltpu.CompilerParams(vmem_limit_by...  7.59 us
  transfers between devices with their start and end apart: 9, of which 6 were waited for; matrix products, arithmetic and copies ran while one was open for 0% of the time, Pallas kernels for 0%

profile of v3, /device:TPU:0, one launch (start us, length us, event | category | flops | bytes accessed | tf_op | source)
XLA Modules:
  0.0 32.1 jit_solution(10654954501606524413)
XLA Ops:
  0.6 0.0 copy-start
  0.6 5.8 %shard_map.86 = (f32[2,7,4,56,128]{4,3,2,1,0:T(8,128)S(1)}, f32[56,512]{1,0:T(8,128)S(1)}, f32[56,512]{1,0:T(8,128)S(1)}, f32[112,128]{1,0:T(8,128)S(1)}, f32[112,128]{1,0:T(8,128)S(1)}) custom-call(s32[1,3]{1,0:T(1,128)} %bitcast.1, f32[7,7,7,512]{3,2,1,0:T(8,128)} %u_in.1, f32[3,8,64]{2,1,0:T(8,128)} %diag_in.1, f32[3,8,64]{2,1,0:T(8,128)} %off_in.1, ...), custom_call_target="tpu_custom_call" | custom-call | flops 1000000000 | bytes 1000000 | tf_op jit(solution)/shard_map/pallas_call | solution.py:377
  6.4 0.5 %collective-permute-start = (f32[56,512]{1,0:T(8,128)S(1)}, f32[56,512]{1,0:T(8,128)S(1)}, u32[]{:S(2)}, u32[]{:S(2)}) collective-permute-start(f32[56,512]{1,0:T(8,128)S(1)} %get-tuple-element.13), channel_id=1, source_target_pairs={{0,8},{8,16},{16,24},{24,0},{1,9},{9,17},{17,25},{25,1},{2,10},{10... | collective-permute-start | bytes 344072 | tf_op jit(solution)/shard_map/ppermute | solution.py:355
  7.0 2.0 %collective-permute-start.1 = (f32[56,512]{1,0:T(8,128)S(1)}, f32[56,512]{1,0:T(8,128)S(1)}, u32[]{:S(2)}, u32[]{:S(2)}) collective-permute-start(f32[56,512]{1,0:T(8,128)S(1)} %get-tuple-element.14), channel_id=1, source_target_pairs={{0,24},{8,0},{16,8},{24,16},{1,25},{9,1},{17,9},{25,17},{2,26},{10... | collective-permute-start | bytes 344072 | tf_op jit(solution)/shard_map/ppermute | solution.py:355
  8.9 2.4 %collective-permute-done.xlow_ref = f32[56,512]{1,0:T(8,128)S(1)} collective-permute-done((f32[56,512]{1,0:T(8,128)S(1)}, f32[56,512]{1,0:T(8,128)S(1)}, u32[]{:S(2)}, u32[]{:S(2)}) %collective-permute-start) | collective-permute-done | bytes 114720 | tf_op jit(solution)/shard_map/ppermute | solution.py:355
  11.4 1.0 %collective-permute-done.1.xhigh_ref = f32[56,512]{1,0:T(8,128)S(1)} collective-permute-done((f32[56,512]{1,0:T(8,128)S(1)}, f32[56,512]{1,0:T(8,128)S(1)}, u32[]{:S(2)}, u32[]{:S(2)}) %collective-permute-start.1) | collective-permute-done | bytes 114720 | tf_op jit(solution)/shard_map/ppermute | solution.py:355
  12.4 0.0 copy-done
  12.4 0.3 shard_map.88
  12.7 1.6 %collective-permute-start.6 = (f32[784,128]{1,0:T(8,128)S(1)}, f32[784,128]{1,0:T(8,128)S(1)}, u32[]{:S(2)}, u32[]{:S(2)}) collective-permute-start(f32[784,128]{1,0:T(8,128)S(1)} %get-tuple-element.19), channel_id=1, source_target_pairs={{0,4},{4,0},{1,5},{5,1},{2,6},{6,2},{3,7},{7,3},{8,12},{12,8},{9,1... | collective-permute-start | bytes 1204232 | tf_op jit(solution)/shard_map/ppermute | solution.py:355
  14.3 1.5 %collective-permute-start.2 = (f32[112,128]{1,0:T(8,128)S(1)}, f32[112,128]{1,0:T(8,128)S(1)}, u32[]{:S(2)}, u32[]{:S(2)}) collective-permute-start(f32[112,128]{1,0:T(8,128)S(1)} %get-tuple-element.15), channel_id=1, source_target_pairs={{0,5},{1,6},{2,7},{3,4},{4,1},{5,2},{6,3},{7,0},{8,13},{9,14},{10,... | collective-permute-start | bytes 172040 | tf_op jit(solution)/shard_map/ppermute | solution.py:355
  15.8 3.2 %collective-permute-start.3 = (f32[112,128]{1,0:T(8,128)S(1)}, f32[112,128]{1,0:T(8,128)S(1)}, u32[]{:S(2)}, u32[]{:S(2)}) collective-permute-start(f32[112,128]{1,0:T(8,128)S(1)} %get-tuple-element.16), channel_id=1, source_target_pairs={{0,7},{1,4},{2,5},{3,6},{4,3},{5,0},{6,1},{7,2},{8,15},{9,12},{10,... | collective-permute-start | bytes 172040 | tf_op jit(solution)/shard_map/ppermute | solution.py:355
  19.0 0.0 collective-permute-start.7
  19.0 3.8 %collective-permute-start.8 = (f32[392,128]{1,0:T(8,128)S(1)}, f32[392,128]{1,0:T(8,128)S(1)}, u32[]{:S(2)}, u32[]{:S(2)}) collective-permute-start(f32[392,128]{1,0:T(8,128)S(1)} %get-tuple-element.21), channel_id=1, source_target_pairs={{0,3},{1,0},{2,1},{3,2},{4,7},{5,4},{6,5},{7,6},{8,11},{9,8},{10,9... | collective-permute-start | bytes 602120 | tf_op jit(solution)/shard_map/ppermute | solution.py:355
  22.8 0.0 collective-permute-done.2.dlow_ref
  22.8 0.0 collective-permute-done.3.dhigh_ref
  22.8 0.1 shard_map.87
  23.0 0.1 collective-permute-start.4
  23.0 1.7 %collective-permute-start.5 = (f32[312,128]{1,0:T(8,128)S(1)}, f32[312,128]{1,0:T(8,128)S(1)}, u32[]{:S(2)}, u32[]{:S(2)}) collective-permute-start(f32[312,128]{1,0:T(8,128)S(1)} %get-tuple-element.18), channel_id=1, source_target_pairs={{0,24},{8,0},{16,8},{24,16},{1,25},{9,1},{17,9},{25,17},{2,26},{10... | collective-permute-start | bytes 479240 | tf_op jit(solution)/shard_map/ppermute | solution.py:355
  24.8 3.0 %collective-permute-done.4.llow_ref = f32[312,128]{1,0:T(8,128)S(1)} collective-permute-done((f32[312,128]{1,0:T(8,128)S(1)}, f32[312,128]{1,0:T(8,128)S(1)}, u32[]{:S(2)}, u32[]{:S(2)}) %collective-permute-start.4) | collective-permute-done | bytes 159776 | tf_op jit(solution)/shard_map/ppermute | solution.py:355
  27.7 0.9 %collective-permute-done.5.lhigh_ref = f32[312,128]{1,0:T(8,128)S(1)} collective-permute-done((f32[312,128]{1,0:T(8,128)S(1)}, f32[312,128]{1,0:T(8,128)S(1)}, u32[]{:S(2)}, u32[]{:S(2)}) %collective-permute-start.5) | collective-permute-done | bytes 159776 | tf_op jit(solution)/shard_map/ppermute | solution.py:355
  28.6 0.1 collective-permute-done.7.zlow_ref
  28.7 2.0 %collective-permute-done.8.zhigh_ref = f32[392,128]{1,0:T(8,128)S(1)} collective-permute-done((f32[392,128]{1,0:T(8,128)S(1)}, f32[392,128]{1,0:T(8,128)S(1)}, u32[]{:S(2)}, u32[]{:S(2)}) %collective-permute-start.8) | collective-permute-done | bytes 200736 | tf_op jit(solution)/shard_map/ppermute | solution.py:355
  30.7 0.0 collective-permute-done.6.y_ref
  30.7 1.4 %shard_map.89 = (f32[7,7,7,512]{3,2,1,0:T(8,128)}, f32[7,7,7,512]{3,2,1,0:T(8,128)}) custom-call(s32[1,3]{1,0:T(1,128)S(1)} %bitcast.4, f32[2,7,4,56,128]{4,3,2,1,0:T(8,128)S(1)} %get-tuple-element.12.bulk_ref, f32[56,512]{1,0:T(8,128)S(1)} %collective-permute-done.xlow_ref, f32[56,512]{1,0:T(8,128)S(1)} %collective-permute-done.1.xhigh_ref, ...), custom_call_target="tpu_custom_call" | custom-call | flops 100000000 | bytes 1000000 | tf_op jit(solution)/shard_map/pallas_call | solution.py:377
Async XLA Ops:
  0.6 11.8 %copy-start = (s32[1,1,1,3]{3,2,1,0:T(1,128)S(1)}, s32[1,1,1,3]{3,2,1,0:T(1,128)}, u32[]{:S(2)}) copy-start(s32[1,1,1,3]{3,2,1,0:T(1,128)} %param.11) | copy-start | bytes 40
  6.4 4.9 %collective-permute-start = (f32[56,512]{1,0:T(8,128)S(1)}, f32[56,512]{1,0:T(8,128)S(1)}, u32[]{:S(2)}, u32[]{:S(2)}) collective-permute-start(f32[56,512]{1,0:T(8,128)S(1)} %get-tuple-element.13), channel_id=1, source_target_pairs={{0,8},{8,16},{16,24},{24,0},{1,9},{9,17},{17,25},{25,1},{2,10},{10... | collective-permute-start | bytes 344072 | tf_op jit(solution)/shard_map/ppermute | solution.py:355
  7.0 5.4 %collective-permute-start.1 = (f32[56,512]{1,0:T(8,128)S(1)}, f32[56,512]{1,0:T(8,128)S(1)}, u32[]{:S(2)}, u32[]{:S(2)}) collective-permute-start(f32[56,512]{1,0:T(8,128)S(1)} %get-tuple-element.14), channel_id=1, source_target_pairs={{0,24},{8,0},{16,8},{24,16},{1,25},{9,1},{17,9},{25,17},{2,26},{10... | collective-permute-start | bytes 344072 | tf_op jit(solution)/shard_map/ppermute | solution.py:355
  12.7 18.0 %collective-permute-start.6 = (f32[784,128]{1,0:T(8,128)S(1)}, f32[784,128]{1,0:T(8,128)S(1)}, u32[]{:S(2)}, u32[]{:S(2)}) collective-permute-start(f32[784,128]{1,0:T(8,128)S(1)} %get-tuple-element.19), channel_id=1, source_target_pairs={{0,4},{4,0},{1,5},{5,1},{2,6},{6,2},{3,7},{7,3},{8,12},{12,8},{9,1... | collective-permute-start | bytes 1204232 | tf_op jit(solution)/shard_map/ppermute | solution.py:355
  14.3 8.6 %collective-permute-start.2 = (f32[112,128]{1,0:T(8,128)S(1)}, f32[112,128]{1,0:T(8,128)S(1)}, u32[]{:S(2)}, u32[]{:S(2)}) collective-permute-start(f32[112,128]{1,0:T(8,128)S(1)} %get-tuple-element.15), channel_id=1, source_target_pairs={{0,5},{1,6},{2,7},{3,4},{4,1},{5,2},{6,3},{7,0},{8,13},{9,14},{10,... | collective-permute-start | bytes 172040 | tf_op jit(solution)/shard_map/ppermute | solution.py:355
  15.8 7.0 %collective-permute-start.3 = (f32[112,128]{1,0:T(8,128)S(1)}, f32[112,128]{1,0:T(8,128)S(1)}, u32[]{:S(2)}, u32[]{:S(2)}) collective-permute-start(f32[112,128]{1,0:T(8,128)S(1)} %get-tuple-element.16), channel_id=1, source_target_pairs={{0,7},{1,4},{2,5},{3,6},{4,3},{5,0},{6,1},{7,2},{8,15},{9,12},{10,... | collective-permute-start | bytes 172040 | tf_op jit(solution)/shard_map/ppermute | solution.py:355
  19.0 9.7 %collective-permute-start.7 = (f32[392,128]{1,0:T(8,128)S(1)}, f32[392,128]{1,0:T(8,128)S(1)}, u32[]{:S(2)}, u32[]{:S(2)}) collective-permute-start(f32[392,128]{1,0:T(8,128)S(1)} %get-tuple-element.20), channel_id=1, source_target_pairs={{0,1},{1,2},{2,3},{3,0},{4,5},{5,6},{6,7},{7,4},{8,9},{9,10},{10,1... | collective-permute-start | bytes 602120 | tf_op jit(solution)/shard_map/ppermute | solution.py:355
  19.0 11.7 %collective-permute-start.8 = (f32[392,128]{1,0:T(8,128)S(1)}, f32[392,128]{1,0:T(8,128)S(1)}, u32[]{:S(2)}, u32[]{:S(2)}) collective-permute-start(f32[392,128]{1,0:T(8,128)S(1)} %get-tuple-element.21), channel_id=1, source_target_pairs={{0,3},{1,0},{2,1},{3,2},{4,7},{5,4},{6,5},{7,6},{8,11},{9,8},{10,9... | collective-permute-start | bytes 602120 | tf_op jit(solution)/shard_map/ppermute | solution.py:355
  23.0 4.8 %collective-permute-start.4 = (f32[312,128]{1,0:T(8,128)S(1)}, f32[312,128]{1,0:T(8,128)S(1)}, u32[]{:S(2)}, u32[]{:S(2)}) collective-permute-start(f32[312,128]{1,0:T(8,128)S(1)} %get-tuple-element.17), channel_id=1, source_target_pairs={{0,8},{8,16},{16,24},{24,0},{1,9},{9,17},{17,25},{25,1},{2,10},{10... | collective-permute-start | bytes 479240 | tf_op jit(solution)/shard_map/ppermute | solution.py:355
  23.0 5.6 %collective-permute-start.5 = (f32[312,128]{1,0:T(8,128)S(1)}, f32[312,128]{1,0:T(8,128)S(1)}, u32[]{:S(2)}, u32[]{:S(2)}) collective-permute-start(f32[312,128]{1,0:T(8,128)S(1)} %get-tuple-element.18), channel_id=1, source_target_pairs={{0,24},{8,0},{16,8},{24,16},{1,25},{9,1},{17,9},{25,17},{2,26},{10... | collective-permute-start | bytes 479240 | tf_op jit(solution)/shard_map/ppermute | solution.py:355
